TPU v7x, 32 devices: a whole 2x2x4 slice. The times are simulated.
32 devices in a mesh: orb: 16 (over z, y, core), grid: 2 (over x).
Axes of the slice: x: 2, y: 2, z: 4, core: 2. Of those that a mesh axis runs over, the one named last changes fastest.
Arguments:
- orbitals: bfloat16 [32, 11520], P('orb', 'grid'), may hold values from -1.5 to 1.5
- occupation: bfloat16 [32], P('orb'), may hold values from 0.29882812 to 1
Outputs:
- potentials: float32 [32, 11520], P('orb', 'grid')
- projectors: float32 [32, 11520], P('orb', 'grid')
All inputs are finite; a program needn't handle non-finite values.
Results may differ from a plain program's by a relative error of at most 0.0025.
Values may be sent and summed in bfloat16 or wider, within the bound.
A program may use at most 64 MiB of HBM per device.

v0:
```python
import math

import jax
import jax.numpy as jnp
from jax import lax
from jax.sharding import PartitionSpec as P

NX = 20
NY = 24
NZ = 24
NPTS = 11520


def hartley_table(length):
    index = jnp.arange(length, dtype=jnp.int32)
    product = index[:, None] * index[None, :] % length
    angle = 2.0 * math.pi / length * product.astype(jnp.float32)
    return (jnp.cos(angle) + jnp.sin(angle)).astype(jnp.bfloat16)


def signed_square(length):
    index = jnp.arange(length, dtype=jnp.int32)
    signed = jnp.where(index <= length // 2, index, index - length).astype(jnp.float32)
    return (2.0 * math.pi * signed / length) ** 2


def coulomb_kernel(size_x, size_y, size_z):
    total = (
        signed_square(size_x)[:, None, None]
        + signed_square(size_y)[None, :, None]
        + signed_square(size_z)[None, None, :]
    )
    safe = jnp.where(total > 0, total, 1.0)
    return jnp.where(total > 0, 1.0 / safe, 0.0) / (size_x * size_y * size_z)


def solve_pairs(density, table_x, table_y, table_z, kernel):
    section = jnp.einsum(
        "ax,pxyz->payz", table_x, density, preferred_element_type=jnp.float32
    ).astype(jnp.bfloat16)
    section = jnp.einsum(
        "by,pxyz->pxbz", table_y, section, preferred_element_type=jnp.float32
    ).astype(jnp.bfloat16)
    spectrum = jnp.einsum("cz,pxyz->pxyc", table_z, section, preferred_element_type=jnp.float32)
    section = (spectrum * kernel).astype(jnp.bfloat16)
    section = jnp.einsum(
        "cz,pxyz->pxyc", table_z, section, preferred_element_type=jnp.float32
    ).astype(jnp.bfloat16)
    section = jnp.einsum(
        "by,pxyz->pxbz", table_y, section, preferred_element_type=jnp.float32
    ).astype(jnp.bfloat16)
    return jnp.einsum("ax,pxyz->payz", table_x, section, preferred_element_type=jnp.float32)


def pair_folder(targets, running, pieces):
    table_x = hartley_table(NX)
    table_y = hartley_table(NY)
    table_z = hartley_table(NZ)
    kernel = coulomb_kernel(NX, NY, NZ)
    target_rows = targets.astype(jnp.float32)
    target_count = targets.shape[0]
    block, block_weight = pieces
    rows = block.shape[0]
    group = math.gcd(rows, 64)
    blocks = block.reshape(rows // group, group, NPTS)
    weights = block_weight.astype(jnp.float32).reshape(rows // group, group)

    def accumulate(totals, inputs):
        sources, source_weight = inputs
        source_rows = sources.astype(jnp.float32)
        density = (target_rows[:, None, :] * source_rows[None, :, :]).astype(jnp.bfloat16)
        density = density.reshape(target_count * group, NX, NY, NZ)
        potential = solve_pairs(density, table_x, table_y, table_z, kernel).reshape(
            target_count, group, NPTS
        )
        weighted = source_weight[None, :, None] * potential * source_rows[None, :, :]
        return (totals - jnp.sum(weighted, axis=1), None)

    result, unused = lax.scan(accumulate, running, (blocks, weights))
    return result


def on_device(orbitals, occupation):
    own_count = orbitals.shape[0]
    per_device = own_count // lax.axis_size("grid")
    empty = jnp.zeros((per_device, NPTS), jnp.float32)
    whole = lax.all_gather(orbitals, "grid", axis=1, tiled=True)
    targets = lax.dynamic_slice_in_dim(whole, lax.axis_index("grid") * per_device, per_device, 0)
    totals = pair_folder(
        targets,
        empty,
        (
            lax.all_gather(whole, "orb", axis=0, tiled=True),
            lax.all_gather(occupation, "orb", axis=0, tiled=True),
        ),
    )
    potentials = lax.all_to_all(totals, "grid", split_axis=1, concat_axis=0, tiled=True)
    source_points, potential_points = (
        lax.all_to_all(
            orbitals.astype(jnp.float32), "orb", split_axis=1, concat_axis=0, tiled=True
        ),
        lax.all_to_all(potentials, "orb", split_axis=1, concat_axis=0, tiled=True),
    )
    partial_gram = (
        lax.dot_general(
            source_points,
            potential_points,
            (((1,), (1,)), ((), ())),
            precision=lax.Precision.HIGHEST,
        )
        / NPTS
    )
    gram = lax.psum(partial_gram, ("orb", "grid"))
    factor = jnp.linalg.cholesky(-gram)
    identity = jnp.eye(gram.shape[0], dtype=jnp.float32)
    inverse = lax.linalg.triangular_solve(factor, identity, left_side=True, lower=True)
    projector_points = jnp.dot(inverse, potential_points, precision=lax.Precision.HIGHEST)
    projectors = lax.all_to_all(projector_points, "orb", split_axis=0, concat_axis=1, tiled=True)
    return (potentials, projectors)


def solution(mesh):
    placed = (P("orb", "grid"), P("orb"))
    return jax.shard_map(
        on_device,
        mesh=mesh,
        in_specs=placed,
        out_specs=(P("orb", "grid"), P("orb", "grid")),
        check_vma=False,
    )
```

profile of v0, /device:TPU:0, one launch (start us, length us, event | category | flops | bytes accessed | tf_op | source)
XLA Modules:
  0.0 226.1 jit_solution(919936937522886090)
XLA Ops:
  0.7 5.7 %all_gather.10 = bf16[2,11520]{1,0:T(2,128)(2,1)S(1)} all-gather(bf16[2,5760]{1,0:T(2,128)(2,1)} %param.2), channel_id=1, replica_groups=mesh['orb'=16,'grid'=2] {'grid'}, dimensions={1}, use_global_device_ids=true | all-gather | bytes 69120 | tf_op jit(solution)/shard_map/all_gather | solution.py:87
  6.3 24.3 %all-gather = bf16[16,2,11520]{2,1,0:T(2,128)(2,1)S(1)} all-gather(bf16[1,2,11520]{2,1,0:T(2,128)(2,1)S(1)} %bitcast.58), channel_id=1, replica_groups=mesh['orb'=16,'grid'=2] {'orb'}, dimensions={0}, use_global_device_ids=true | all-gather | bytes 783360 | tf_op jit(solution)/shard_map/all_gather | solution.py:93
  30.7 6.4 %reshape.167 = f32[32,20,24,24]{3,2,1,0:T(8,128)} reshape(bf16[16,2,11520]{2,1,0:T(2,128)(2,1)S(1)} %all-gather) | data formatting | bytes 2211840 | tf_op jit(solution)/shard_map/while/body/eval_jaxpr/convert_element_type | solution.py:70
  38.8 3.9 %multiply_convert_fusion.1 = bf16[32,20,24,24]{3,2,1,0:T(8,128)(2,1)S(1)} fusion(f32[32,20,24,24]{3,2,1,0:T(8,128)} %reshape.167, f32[20,24,24]{2,1,0:T(8,128)S(1)} %reshape.166), kind=kLoop, calls=%fused_computation.1 | loop fusion | flops 737280 | bytes 2257920 | tf_op jit(solution)/shard_map/while/body/eval_jaxpr/convert_element_type | solution.py:71
  42.6 4.9 %convert_bitcast_fusion = bf16[32,20,24,24]{1,3,2,0:T(8,128)(2,1)} fusion(bf16[32,20,24,24]{3,2,1,0:T(8,128)(2,1)S(1)} %multiply_convert_fusion.1), kind=kOutput, calls=%fused_computation.4 | convolution fusion | flops 15118640 | bytes 1474560 | tf_op jit(solution)/shard_map/while/body/eval_jaxpr/ax,pxyz->payz/dot_general | solution.py:38
  47.5 8.5 %copy.24 = bf16[32,20,24,24]{2,3,1,0:T(8,128)(2,1)} copy(bf16[32,20,24,24]{1,3,2,0:T(8,128)(2,1)} %convert_bitcast_fusion) | data formatting | bytes 1474560 | tf_op jit(solution)/shard_map/while/body/eval_jaxpr/convert_element_type | solution.py:40
  56.0 5.2 %fusion.44 = bf16[32,20,24,24]{3,2,1,0:T(8,128)(2,1)} fusion(bf16[32,20,24,24]{2,3,1,0:T(8,128)(2,1)} %copy.24), kind=kOutput, calls=%fused_computation.53 | convolution fusion | flops 17701056 | bytes 1474560 | tf_op jit(solution)/shard_map/while/body/eval_jaxpr/by,pxyz->pxbz/dot_general | solution.py:41
  61.5 7.4 %fusion.2 = bf16[32,20,24,24]{3,2,1,0:T(8,128)(2,1)} fusion(f32[20,24,24]{2,1,0:T(8,128)S(1)} %fusion.19, bf16[32,20,24,24]{3,2,1,0:T(8,128)(2,1)} %fusion.44), kind=kOutput, calls=%fused_computation.5 | convolution fusion | flops 36139392 | bytes 1520640 | tf_op jit(solution)/shard_map/while/body/eval_jaxpr/cz,pxyz->pxyc/dot_general | solution.py:46
  68.9 5.4 %convert_bitcast_fusion.1 = bf16[32,20,24,24]{2,3,1,0:T(8,128)(2,1)} fusion(bf16[32,20,24,24]{3,2,1,0:T(8,128)(2,1)} %fusion.2), kind=kOutput, calls=%fused_computation.8 | convolution fusion | flops 18069696 | bytes 1474560 | tf_op jit(solution)/shard_map/while/body/eval_jaxpr/by,pxyz->pxbz/dot_general | solution.py:49
  74.3 10.1 %copy.27 = bf16[32,20,24,24]{0,1,3,2:T(8,128)(2,1)S(1)} copy(bf16[32,20,24,24]{2,3,1,0:T(8,128)(2,1)} %convert_bitcast_fusion.1) | data formatting | bytes 1474560 | tf_op jit(solution)/shard_map/while/body/eval_jaxpr/convert_element_type | solution.py:51
  84.4 4.0 %convolution_bitcast_fusion = f32[32,20,24,24]{0,1,3,2:T(8,128)} fusion(bf16[32,20,24,24]{0,1,3,2:T(8,128)(2,1)S(1)} %copy.27), kind=kOutput, calls=%fused_computation.13 | convolution fusion | flops 14750000 | bytes 2211840 | tf_op jit(solution)/shard_map/while/body/eval_jaxpr/ax,pxyz->payz/dot_general | solution.py:52
  88.4 12.1 %copy.28 = f32[32,20,24,24]{3,2,1,0:T(8,128)} copy(f32[32,20,24,24]{0,1,3,2:T(8,128)} %convolution_bitcast_fusion) | data formatting | bytes 2949120 | tf_op jit(solution)/shard_map/while/body/eval_jaxpr/ax,pxyz->payz/transpose | solution.py:52
  102.0 6.8 %reshape.165 = f32[32,11520]{1,0:T(8,128)S(1)} reshape(f32[32,20,24,24]{3,2,1,0:T(8,128)} %copy.28) | data formatting | bytes 2949120 | tf_op jit(solution)/shard_map/while/body/eval_jaxpr/reshape | solution.py:73
  108.9 29.9 %all-reduce = bf16[32]{0:T(256)(128)(2,1)S(1)} all-reduce(bf16[32]{0:T(256)(128)(2,1)S(1)} %dynamic-update-slice.3), channel_id=1, replica_groups=mesh['orb'=16,'grid'=2] {'orb'}, use_global_device_ids=true, to_apply=%add | all-reduce | flops 32 | bytes 128
  139.7 3.3 %all-to-all-start = ((f32[1,2,5760]{2,0,1:T(1,128)}), f32[1,2,5760]{2,0,1:T(1,128)S(1)}, u32[]{:S(2)}, u32[]{:S(2)}) async-start(f32[1,2,5760]{2,0,1:T(1,128)} %sub.25), calls=%async_computation | async-start | bytes 92160 | tf_op jit(solution)/shard_map/all_to_all | solution.py:97
  143.8 3.2 %all-to-all-done = f32[1,2,5760]{2,0,1:T(1,128)S(1)} async-done(((f32[1,2,5760]{2,0,1:T(1,128)}), f32[1,2,5760]{2,0,1:T(1,128)S(1)}, u32[]{:S(2)}, u32[]{:S(2)}) %all-to-all-start) | async-done | bytes 46112 | tf_op jit(solution)/shard_map/all_to_all | solution.py:97
  147.0 3.5 %all-to-all-start.2 = ((f32[2,16,360]{2,0,1:T(2,128)}), f32[2,16,360]{2,0,1:T(2,128)S(1)}, u32[]{:S(2)}, u32[]{:S(2)}) async-start(f32[2,16,360]{2,0,1:T(2,128)} %copy.30), calls=%async_computation.2 | async-start | bytes 98304 | tf_op jit(solution)/shard_map/all_to_all | solution.py:99
  151.4 5.8 %all-to-all-done.2 = f32[2,16,360]{2,0,1:T(2,128)S(1)} async-done(((f32[2,16,360]{2,0,1:T(2,128)}), f32[2,16,360]{2,0,1:T(2,128)S(1)}, u32[]{:S(2)}, u32[]{:S(2)}) %all-to-all-start.2) | async-done | bytes 46112 | tf_op jit(solution)/shard_map/all_to_all | solution.py:99
  157.3 3.5 %all-to-all-start.1 = ((f32[2,16,360]{2,0,1:T(2,128)}), f32[2,16,360]{2,0,1:T(2,128)S(1)}, u32[]{:S(2)}, u32[]{:S(2)}) async-start(f32[2,16,360]{2,0,1:T(2,128)} %copy.29), calls=%async_computation.1 | async-start | bytes 98304 | tf_op jit(solution)/shard_map/all_to_all | solution.py:102
  160.8 6.7 %all-to-all-done.1 = f32[2,16,360]{2,0,1:T(2,128)S(1)} async-done(((f32[2,16,360]{2,0,1:T(2,128)}), f32[2,16,360]{2,0,1:T(2,128)S(1)}, u32[]{:S(2)}, u32[]{:S(2)}) %all-to-all-start.1) | async-done | bytes 46112 | tf_op jit(solution)/shard_map/all_to_all | solution.py:102
  167.8 38.0 %psum.7 = f32[32,32]{0,1:T(8,128)S(1)} all-reduce(f32[32,32]{0,1:T(8,128)S(1)} %fusion.17), channel_id=1, replica_groups=mesh['orb'=16,'grid'=2] {'orb','grid'}, use_global_device_ids=true, to_apply=%region_1.2 | all-reduce | flops 1024 | bytes 8192 | tf_op jit(solution)/shard_map/psum | solution.py:113
  205.8 2.9 %cholesky.17 = f32[32,32]{1,0:T(8,128)S(1)} custom-call(f32[32,32]{1,0:T(8,128)S(1)} %fusion.22), custom_call_target="Cholesky" | custom-call | tf_op jit(solution)/shard_map/jit(cholesky)/cholesky | solution.py:114
  213.6 5.0 %all-to-all-start.3 = ((f32[16,2,360]{2,1,0:T(2,128)}), f32[16,2,360]{2,1,0:T(2,128)S(1)}, u32[]{:S(2)}, u32[]{:S(2)}) async-start(f32[16,2,360]{2,1,0:T(2,128)} %copy.34), calls=%async_computation.3 | async-start | bytes 98304 | tf_op jit(solution)/shard_map/all_to_all | solution.py:118
  219.3 6.1 %all-to-all-done.3 = f32[16,2,360]{2,1,0:T(2,128)S(1)} async-done(((f32[16,2,360]{2,1,0:T(2,128)}), f32[16,2,360]{2,1,0:T(2,128)S(1)}, u32[]{:S(2)}, u32[]{:S(2)}) %all-to-all-start.3) | async-done | bytes 46112 | tf_op jit(solution)/shard_map/all_to_all | solution.py:118
  (45 shorter events, 11.9 us)
Async XLA Ops:
  88.4 12.1 %copy-start.3 = (u32[32]{0:T(128)S(1)}, u32[32]{0:T(128)}, u32[]{:S(2)}) copy-start(u32[32]{0:T(128)} %constant.125) | copy-start | bytes 388
  88.4 13.4 %copy-start.2 = (bf16[2]{0:T(256)(128)(2,1)S(1)}, bf16[2]{0:T(256)(128)(2,1)}, u32[]{:S(2)}) copy-start(bf16[2]{0:T(256)(128)(2,1)} %param.3) | copy-start | bytes 16
  102.0 36.7 %copy-start = (f32[32,11520]{1,0:T(8,128)S(1)}, f32[32,11520]{1,0:T(8,128)}, u32[]{:S(2)}) copy-start(f32[32,11520]{1,0:T(8,128)} %reshape.174) | copy-start | bytes 4423684
  102.0 41.0 %copy-start.1 = (bf16[2,5760]{1,0:T(2,128)(2,1)S(1)}, bf16[2,5760]{1,0:T(2,128)(2,1)}, u32[]{:S(2)}) copy-start(bf16[2,5760]{1,0:T(2,128)(2,1)} %param.2) | copy-start | bytes 69124
  139.7 7.3 %all-to-all-start = ((f32[1,2,5760]{2,0,1:T(1,128)}), f32[1,2,5760]{2,0,1:T(1,128)S(1)}, u32[]{:S(2)}, u32[]{:S(2)}) async-start(f32[1,2,5760]{2,0,1:T(1,128)} %sub.25), calls=%async_computation | async-start | bytes 92160 | tf_op jit(solution)/shard_map/all_to_all | solution.py:97
  147.0 10.2 %all-to-all-start.2 = ((f32[2,16,360]{2,0,1:T(2,128)}), f32[2,16,360]{2,0,1:T(2,128)S(1)}, u32[]{:S(2)}, u32[]{:S(2)}) async-start(f32[2,16,360]{2,0,1:T(2,128)} %copy.30), calls=%async_computation.2 | async-start | bytes 98304 | tf_op jit(solution)/shard_map/all_to_all | solution.py:99
  157.3 10.2 %all-to-all-start.1 = ((f32[2,16,360]{2,0,1:T(2,128)}), f32[2,16,360]{2,0,1:T(2,128)S(1)}, u32[]{:S(2)}, u32[]{:S(2)}) async-start(f32[2,16,360]{2,0,1:T(2,128)} %copy.29), calls=%async_computation.1 | async-start | bytes 98304 | tf_op jit(solution)/shard_map/all_to_all | solution.py:102
  213.6 11.8 %all-to-all-start.3 = ((f32[16,2,360]{2,1,0:T(2,128)}), f32[16,2,360]{2,1,0:T(2,128)S(1)}, u32[]{:S(2)}, u32[]{:S(2)}) async-start(f32[16,2,360]{2,1,0:T(2,128)} %copy.34), calls=%async_computation.3 | async-start | bytes 98304 | tf_op jit(solution)/shard_map/all_to_all | solution.py:118
where the time goes:
time: 227 us; the launch traced here: 226 us
  blocking collectives  97.9 us (43%)
  local copies, waits for them, and re-layouts  50.8 us (22%)
  matrix products  27.5 us (12%)
  waiting for transfers between devices  21.9 us (10%)
  starting transfers between devices  15.3 us (7%)
  other arithmetic  11.4 us (5%)
    psum x1, blocking collectives, on_device(): gram = lax.psum(partial_gram, ('orb', 'grid'))  38 us
    unnamed x1, blocking collectives  29.9 us
    all_gather x1, blocking collectives, on_device(): lax.all_gather(whole, 'orb', axis=0, tiled=True)  24.3 us
    transpose x1, local copies, waits for them, and re-layouts, solve_pairs(): jnp.einsum('ax,pxyz->payz', table_x, section, preferred_element_type=jnp....  12.1 us
    dot_general x2, matrix products, solve_pairs(): jnp.einsum('by,pxyz->pxbz', table_y, section, preferred_element_type=jnp....  10.6 us
    convert_element_type x1, local copies, waits for them, and re-layouts, solve_pairs(): section = jnp.einsum('by,pxyz->pxbz', table_y, section, preferred_element...  10.1 us
    convert_element_type x1, local copies, waits for them, and re-layouts, solve_pairs(): section = jnp.einsum('ax,pxyz->payz', table_x, density, preferred_element...  8.51 us
    convert_element_type x2, local copies, waits for them, and re-layouts, accumulate(): source_rows = sources.astype(jnp.float32)  7.76 us
  transfers between devices with their start and end apart: 4, of which 4 were waited for; matrix products, arithmetic and copies ran while one was open for 1% of the time, Pallas kernels for 0%

commit v1 on v0

v1 whole, which is shorter than its diff:
```python
import functools
import math

import jax
import jax.numpy as jnp
import numpy as np
from jax import lax
from jax.experimental import pallas as pl
from jax.experimental.pallas import tpu as pltpu
from jax.sharding import PartitionSpec as P

NX = 20
NY = 24
NZ = 24
NPTS = NX * NY * NZ
PLANE = NY * NZ
HALVES = 2
HX = NX // HALVES
ROWS = 16
BATCH = 8
MESH = pl.DeviceIdType.MESH


def hartley_table(length):
    index = np.arange(length, dtype=np.int32)
    product = index[:, None] * index[None, :] % length
    angle = np.float32(2.0 * math.pi / length) * product.astype(np.float32)
    return np.cos(angle) + np.sin(angle)


def signed_square(length):
    index = np.arange(length, dtype=np.int32)
    signed = np.where(index <= length // 2, index, index - length).astype(np.float32)
    return (np.float32(2.0 * math.pi) * signed / np.float32(length)) ** 2


def padded_rows(array):
    halves = array.reshape((HALVES, HX) + array.shape[1:])
    pad = [(0, 0), (0, ROWS - HX)] + [(0, 0)] * (array.ndim - 1)
    return np.pad(halves, pad).reshape((HALVES * ROWS,) + array.shape[1:])


def tables():
    table_x = padded_rows(padded_rows(hartley_table(NX)).T)
    table_x = np.kron(np.eye(BATCH, dtype=np.float32), table_x)
    table_y = np.kron(hartley_table(NY), np.eye(NZ, dtype=np.float32))
    table_z = np.kron(np.eye(16, dtype=np.float32), hartley_table(NZ))
    total = (
        signed_square(NX)[:, None, None]
        + signed_square(NY)[None, :, None]
        + signed_square(NZ)[None, None, :]
    )
    safe = np.where(total > 0, total, 1.0)
    kernel = np.where(total > 0, 1.0 / safe, 0.0) / NPTS
    kernel = padded_rows(kernel.reshape(NX, PLANE).astype(np.float32))
    return (
        jnp.asarray(table_x, jnp.bfloat16),
        jnp.asarray(table_y, jnp.bfloat16),
        jnp.asarray(table_z, jnp.bfloat16),
        jnp.asarray(kernel, jnp.float32),
    )


def column_of(matrix, k):
    if isinstance(k, int):
        return matrix[:, k : k + 1]
    lane = lax.broadcasted_iota(jnp.int32, matrix.shape, 1)
    return jnp.sum(jnp.where(lane == k, matrix, 0.0), axis=1, keepdims=True)


def row_of(matrix, k):
    if isinstance(k, int):
        return matrix[k : k + 1, :]
    line = lax.broadcasted_iota(jnp.int32, matrix.shape, 0)
    return jnp.sum(jnp.where(line == k, matrix, 0.0), axis=0, keepdims=True)


def loop(count, body, carry, most=64):
    if count <= most:
        for k in range(count):
            carry = body(k, carry)
        return carry
    return lax.fori_loop(0, count, body, carry)


def body(
    cols,
    own_ref,
    tx_ref,
    ty_ref,
    tz_ref,
    k_ref,
    pot_ref,
    proj_ref,
    src,
    part,
    part_in,
    pots,
    rowsum,
    gown,
    gall,
    gmat,
    s_a,
    s_y,
    s_c,
    s_x,
    s_cx,
    r_in,
    r_x,
    s_p,
    r_p,
    s_g,
    r_g,
    t_a,
    t_y,
    t_c,
    t_in,
):
    o = lax.axis_index("orb")
    g = lax.axis_index("grid")
    n_orb = 4 * cols
    n = 2 * n_orb
    r = o // 4
    y = (o % 4) // 2
    c = o % 2
    h = 1 - g
    f32 = jnp.float32
    o_y = r * 4 + (1 - y) * 2 + c
    o_c = r * 4 + y * 2 + (1 - c)

    barrier = pltpu.get_barrier_semaphore()

    @pl.loop(1, 2 * n_orb)
    def _(d):
        flat = (o * 2 + g + d) % (2 * n_orb)
        pl.semaphore_signal(
            barrier, inc=1, device_id=(flat // 2, flat % 2), device_id_type=MESH
        )

    pl.semaphore_wait(barrier, 2 * n_orb - 1)

    def copy(source, target, send, recv, orb, grid):
        return pltpu.make_async_remote_copy(
            src_ref=source,
            dst_ref=target,
            send_sem=send,
            recv_sem=recv,
            device_id=(orb, grid),
            device_id_type=MESH,
        )

    def to_column(d, source, target, send, recv):
        q = (r + d) % cols
        return copy(source, target, send.at[q], recv.at[r, y, c], q * 4 + y * 2 + c, g)

    @pl.loop(1, cols)
    def _(d):
        to_column(d, own_ref, src.at[r, y, c, g], s_a, r_in).start()

    copy(own_ref, src.at[r, y, c, g], s_y.at[r], r_in.at[r, y, c], o_y, g).start()
    copy(own_ref, src.at[r, y, c, g], s_x.at[r, y], r_x.at[r, y, c], o, h).start()
    copy(own_ref, src.at[r, y, c, g], s_c.at[r, y], r_in.at[r, y, c], o_c, g).start()
    src[r, y, c, g] = own_ref[...]

    def wait_block(ref, recv):
        copy(ref, ref, s_a.at[r], recv, o_c, g).wait_recv()

    def forward_x(q, u):
        return copy(
            src.at[q, u, c, g, h], src.at[q, u, c, g, h], s_x.at[q, u], r_x.at[q, u, c], o, h
        )

    def forward_c(q, u):
        return copy(
            src.at[q, u, c, g], src.at[q, u, c, g], s_c.at[q, u], r_in.at[q, u, c], o_c, g
        )

    def forward_y(q):
        return copy(src.at[q, y, c, g], src.at[q, y, c, g], s_y.at[q], r_in.at[q, y, c], o_y, g)

    def forward_cx(q, u):
        return copy(
            src.at[q, u, c, h, g], src.at[q, u, c, h, g], s_cx.at[q, u], r_x.at[q, u, c], o_c, g
        )

    @pl.loop(1, cols)
    def _(d):
        q = (r + d) % cols
        wait_block(src.at[q, y, c, g], r_in.at[q, y, c])
        forward_y(q).start()
        forward_x(q, y).start()
        forward_c(q, y).start()

    @pl.loop(0, cols)
    def _(d):
        q = (r + d) % cols
        wait_block(src.at[q, 1 - y, c, g], r_in.at[q, 1 - y, c])
        forward_x(q, 1 - y).start()
        forward_c(q, 1 - y).start()

    wait_block(src.at[r, y, c, h], r_x.at[r, y, c])
    forward_cx(r, y).start()

    @pl.loop(1, cols)
    def _(d):
        q = (r + d) % cols
        wait_block(src.at[q, y, c, h, g], r_x.at[q, y, c])
        forward_cx(q, y).start()

    @pl.loop(0, cols)
    def _(d):
        q = (r + d) % cols
        wait_block(src.at[q, 1 - y, c, h, g], r_x.at[q, 1 - y, c])
        forward_cx(q, 1 - y).start()

    tx = tx_ref[...]
    ty = ty_ref[...]
    tz = tz_ref[...]
    cut = tz.shape[0]
    rest = PLANE - cut
    kern = k_ref[...]

    def mm(a, b):
        return jnp.dot(a, b, preferred_element_type=f32)

    def along_z(a):
        return jnp.concatenate([mm(a[:, :cut], tz), mm(a[:, cut:], tz[:rest, :rest])], axis=1)

    per = BATCH // 2
    block = (BATCH, HALVES * ROWS, PLANE)
    flat_block = (BATCH * HALVES * ROWS, PLANE)

    def one_batch(core, step, first):
        raw = src[pl.ds(step * per, per), :, core, :, g].reshape(block).astype(f32)
        weight = raw[:, HX : HX + 1, :]
        for t in range(2):
            target = src[r, y, c, :, t].reshape(block[1:]).astype(f32)
            density = (raw * target[None]).astype(jnp.bfloat16).reshape(flat_block)
            s = mm(tx, density).astype(jnp.bfloat16)
            s = mm(s, ty).astype(jnp.bfloat16)
            s = along_z(s).reshape(block) * kern[None]
            s = along_z(s.reshape(flat_block).astype(jnp.bfloat16)).astype(jnp.bfloat16)
            s = mm(s, ty).astype(jnp.bfloat16)
            v = mm(tx, s).reshape(block)
            total = jnp.sum(weight * v * raw, axis=0).reshape(HALVES, ROWS, PLANE)
            if first:
                part[:, t] = -total
            else:
                part[:, t] -= total

    one_batch(c, 0, True)
    steps = cols // per
    if steps > 1:

        @pl.loop(1, steps)
        def _(k):
            one_batch(c, k, False)

    @pl.loop(0, cols)
    def _(q):
        for u in range(2):
            wait_block(src.at[q, u, 1 - c, g], r_in.at[q, u, 1 - c])
            wait_block(src.at[q, u, 1 - c, h, g], r_x.at[q, u, 1 - c])

    @pl.loop(0, steps)
    def _(k):
        one_batch(1 - c, k, False)

    swap = copy(part.at[h], part_in, s_p, r_p, o, h)
    swap.start()
    swap.wait_recv()
    final = part[g] + part_in[...]
    pot_ref[...] = final
    pots[r, y, c] = final

    @pl.loop(1, cols)
    def _(d):
        to_column(d, pot_ref, pots.at[r, y, c], t_a, t_in).start()

    copy(pot_ref, pots.at[r, y, c], t_y.at[r], t_in.at[r, y, c], o_y, g).start()
    copy(pot_ref, pots.at[r, y, c], t_c.at[r, y], t_in.at[r, y, c], o_c, g).start()

    @pl.loop(0, cols)
    def _(q):
        rows = src[q, :, :, g].reshape(8, ROWS, PLANE).astype(f32)
        for t in range(2):
            rowsum[t, pl.ds(pl.multiple_of(q * 8, 8), 8), :] = jnp.sum(
                rows * final[t][None], axis=1
            )

    ones = jnp.ones((8, PLANE), f32)

    def lane_sums(t):
        return lax.dot_general(
            ones,
            rowsum[t],
            (((1,), (1,)), ((), ())),
            precision=lax.Precision.HIGHEST,
            preferred_element_type=f32,
        )

    line = lax.broadcasted_iota(jnp.int32, (8, n), 0)
    gown[...] = jnp.where(line == 0, lane_sums(0), lane_sums(1))
    gall[g, o] = gown[...]

    def gram_to(d):
        flat = (o * 2 + g + d) % (2 * n_orb)
        return copy(gown, gall.at[g, o], s_g.at[d], r_g.at[g, o], flat // 2, flat % 2)

    @pl.loop(1, 2 * n_orb)
    def _(d):
        gram_to(d).start()

    def pass_y(q):
        return copy(pots.at[q, y, c], pots.at[q, y, c], t_y.at[q], t_in.at[q, y, c], o_y, g)

    def pass_c(q, u):
        return copy(pots.at[q, u, c], pots.at[q, u, c], t_c.at[q, u], t_in.at[q, u, c], o_c, g)

    @pl.loop(1, cols)
    def _(d):
        q = (r + d) % cols
        wait_block(pots.at[q, y, c], t_in.at[q, y, c])
        pass_y(q).start()
        pass_c(q, y).start()

    @pl.loop(1, 2 * n_orb)
    def _(d):
        flat = (o * 2 + g + d) % (2 * n_orb)
        wait_block(gall.at[flat % 2, flat // 2], r_g.at[flat % 2, flat // 2])

    @pl.loop(0, cols)
    def _(d):
        q = (r + d) % cols
        wait_block(pots.at[q, 1 - y, c], t_in.at[q, 1 - y, c])
        pass_c(q, 1 - y).start()

    def assemble(k, carry):
        pairs = [gall[0, 4 * k + j, 0:2, :] + gall[1, 4 * k + j, 0:2, :] for j in range(4)]
        start = 8 * k if isinstance(k, int) else pl.multiple_of(8 * k, 8)
        gmat[pl.ds(start, 8), :] = jnp.concatenate(pairs, axis=0)
        return carry

    loop(cols, assemble, 0, 16)
    gram = gmat[...]
    sym = (gram + gram.T) * f32(-0.5 / NPTS)
    row_id = lax.broadcasted_iota(jnp.int32, (n, n), 0)
    eye = (row_id == lax.broadcasted_iota(jnp.int32, (n, n), 1)).astype(f32)
    below = lax.broadcasted_iota(jnp.int32, (n, 1), 0)

    def eliminate(k, pair):
        left, right = pair
        row_l = row_of(left, k)
        scale = 1.0 / column_of(row_l, k)
        factor = jnp.where(below > k, column_of(left, k) * scale, 0.0)
        return left - factor * row_l, right - factor * row_of(right, k)

    left, right = loop(n, eliminate, (sym, eye))
    diag = jnp.sum(left * eye, axis=1, keepdims=True)
    inverse = right * (1.0 / jnp.sqrt(diag))
    a0, a1 = row_of(inverse, 2 * o), row_of(inverse, 2 * o + 1)

    @pl.loop(0, cols)
    def _(q):
        for u in range(2):
            wait_block(pots.at[q, u, 1 - c], t_in.at[q, u, 1 - c])

    def add(k, sums):
        p0, p1 = sums
        if isinstance(k, int):
            value = pots[k // 8, (k % 8) // 4, (k % 4) // 2, k % 2]
        else:
            value = pots[k // 8, lax.rem(k, 8) // 4, lax.rem(k, 4) // 2, lax.rem(k, 2)]
        return p0 + column_of(a0, k) * value, p1 + column_of(a1, k) * value

    zero = jnp.zeros((ROWS, PLANE), f32)
    p0, p1 = loop(n, add, (zero, zero))
    proj_ref[0] = p0
    proj_ref[1] = p1

    @pl.loop(1, cols)
    def _(d):
        to_column(d, own_ref, src.at[r, y, c, g], s_a, r_in).wait_send()
        to_column(d, pot_ref, pots.at[r, y, c], t_a, t_in).wait_send()
        q = (r + d) % cols
        forward_x(q, y).wait_send()

    copy(own_ref, src.at[r, y, c, g], s_x.at[r, y], r_x.at[r, y, c], o, h).wait_send()
    swap.wait_send()

    @pl.loop(0, cols)
    def _(q):
        forward_x(q, 1 - y).wait_send()
        forward_y(q).wait_send()
        pass_y(q).wait_send()
        for u in range(2):
            forward_c(q, u).wait_send()
            forward_cx(q, u).wait_send()
            pass_c(q, u).wait_send()

    @pl.loop(1, 2 * n_orb)
    def _(d):
        gram_to(d).wait_send()


def on_device(orbitals, occupation):
    n_orb = lax.axis_size("orb")
    cols = n_orb // 4
    n = 2 * n_orb
    own = orbitals.reshape(2, HX, PLANE)
    weight = jnp.broadcast_to(occupation[:, None, None], (2, 1, PLANE))
    fill = jnp.zeros((2, ROWS - HX - 1, PLANE), jnp.bfloat16)
    own = jnp.concatenate([own, weight, fill], axis=1)
    table_x, table_y, table_z, kernel = tables()
    f32 = jnp.float32
    dma = pltpu.SemaphoreType.DMA
    full = jax.ShapeDtypeStruct((2, ROWS, PLANE), f32)
    pot, proj = pl.pallas_call(
        functools.partial(body, cols),
        out_shape=(full, full),
        in_specs=[pl.BlockSpec(memory_space=pltpu.VMEM)] * 5,
        out_specs=[pl.BlockSpec(memory_space=pltpu.VMEM)] * 2,
        scratch_shapes=[
            pltpu.VMEM((cols, 2, 2, 2, 2, ROWS, PLANE), jnp.bfloat16),
            pltpu.VMEM((2, 2, ROWS, PLANE), f32),
            pltpu.VMEM((2, ROWS, PLANE), f32),
            pltpu.VMEM((cols, 2, 2, 2, ROWS, PLANE), f32),
            pltpu.VMEM((2, n, PLANE), f32),
            pltpu.VMEM((8, n), f32),
            pltpu.VMEM((2, n_orb, 8, n), f32),
            pltpu.VMEM((n, n), f32),
            dma((cols,)),
            dma((cols,)),
            dma((cols, 2)),
            dma((cols, 2)),
            dma((cols, 2)),
            dma((cols, 2, 2)),
            dma((cols, 2, 2)),
            dma,
            dma,
            dma((2 * n_orb,)),
            dma((2, n_orb)),
            dma((cols,)),
            dma((cols,)),
            dma((cols, 2)),
            dma((cols, 2, 2)),
        ],
        compiler_params=pltpu.CompilerParams(
            collective_id=0, has_side_effects=True, vmem_limit_bytes=60 * 1024 * 1024
        ),
        name="exchange",
    )(own, table_x, table_y, table_z, kernel)

    def flat(a):
        return a[:, :HX, :].reshape(2, HX * PLANE)

    return flat(pot), flat(proj)


def solution(mesh):
    return jax.shard_map(
        on_device,
        mesh=mesh,
        in_specs=(P("orb", "grid"), P("orb")),
        out_specs=(P("orb", "grid"), P("orb", "grid")),
        check_vma=False,
    )
```

time: 227 us -> 50.8 us (0.22)
  blocking collectives: 97.9 us -> 0 us
  local copies, waits for them, and re-layouts: 50.8 us -> 3.93 us
  Pallas kernels: 0 us -> 45.2 us
  matrix products: 27.5 us -> 0 us
  waiting for transfers between devices: 21.9 us -> 0 us
  starting transfers between devices: 15.3 us -> 0 us
  other arithmetic: 11.4 us -> 0.69 us
    pallas_call x0 -> x1, Pallas kernels: none -> 45.2 us  [on_device(): pl.pallas_call(functools.partial(body, cols), out_shape=(full, full), in_...]
    psum x1 -> x0, blocking collectives: 38 us -> none  [on_device(): gram = lax.psum(partial_gram, ('orb', 'grid'))]
    all_gather x2 -> x0, blocking collectives: 30 us -> none  [the longest x1 24.3 us: on_device(): lax.all_gather(whole, 'orb', axis=0, tiled=True)]
    unnamed x1 -> x0, blocking collectives: 29.9 us -> none
    dot_general x7 -> x0, matrix products: 27.3 us -> none  [the longest x2 10.6 us: solve_pairs(): jnp.einsum('by,pxyz->pxbz', table_y, section, preferred_element_type=jnp....]
    convert_element_type x4 -> x0, local copies, waits for them, and re-layouts: 26.4 us -> none  [the longest x1 10.1 us: solve_pairs(): section = jnp.einsum('by,pxyz->pxbz', table_y, section, preferred_element...]
    all_to_all x4 -> x0, waiting for transfers between devices: 21.9 us -> none  [the longest x1 6.68 us: on_device(): lax.all_to_all(potentials, 'orb', split_axis=1, concat_axis=0, tiled=True)]
    all_to_all x4 -> x0, starting transfers between devices: 15.3 us -> none  [the longest x1 5 us: on_device(): lax.all_to_all(projector_points, 'orb', split_axis=0, concat_axis=1, tile...]
  transfers between devices with their start and end apart: 4 -> 0, of which waited for: 4 -> 0; matrix products, arithmetic and copies ran while one was open for 1% -> 0% of each run, Pallas kernels for 0% -> 0%
where the time goes in v1:
time: 50.8 us; the launch traced here: 50.5 us
  Pallas kernels  45.2 us (89%)
  local copies, waits for them, and re-layouts  3.93 us (8%)
  other arithmetic  0.69 us (1%)
  between operations  0.67 us (1%)
    pallas_call x1, Pallas kernels, on_device(): pl.pallas_call(functools.partial(body, cols), out_shape=(full, full), in_...  45.2 us
    reshape x2, local copies, waits for them, and re-layouts, flat(): return a[:, :HX, :].reshape(2, HX * PLANE)  2.36 us

profile of v1, /device:TPU:0, one launch (start us, length us, event | category | flops | bytes accessed | tf_op | source)
XLA Modules:
  0.0 50.5 jit_solution(10903183921559503459)
XLA Ops:
  0.6 0.0 copy-start.1
  0.7 0.1 pad.2.clone
  0.7 0.6 %copy-done.1 = bf16[2]{0:T(256)(128)(2,1)S(1)} copy-done((bf16[2]{0:T(256)(128)(2,1)S(1)}, bf16[2]{0:T(256)(128)(2,1)}, u32[]{:S(2)}) %copy-start.1) | copy-done | bytes 28
  1.3 0.1 broadcast_in_dim.4
  1.4 0.8 %reshape.16 = bf16[2,10,576]{2,1,0:T(8,128)(2,1)S(1)} reshape(bf16[2,5760]{1,0:T(2,128)(2,1)} %param.6) | data formatting | bytes 46080 | tf_op jit(solution)/shard_map/reshape | solution.py:410
  2.2 0.7 %maximum_maximum_fusion.own_ref = bf16[2,16,576]{2,1,0:T(8,128)(2,1)} fusion(bf16[2,1,576]{2,1,0:T(2,128)(2,1)S(1)} %broadcast_in_dim.4, bf16[2,10,576]{2,1,0:T(8,128)(2,1)S(1)} %reshape.16, bf16[16]{0:T(256)(128)(2,1)S(1)} %pad.2.clone), kind=kLoop, calls=%fused_computation | loop fusion | flops 110592 | bytes 62240 | tf_op jit(solution)/shard_map/concatenate | solution.py:413
  2.9 45.2 %exchange.1 = (f32[2,16,576]{2,1,0:T(8,128)}, f32[2,16,576]{2,1,0:T(8,128)}) custom-call(bf16[2,16,576]{2,1,0:T(8,128)(2,1)} %maximum_maximum_fusion.own_ref, bf16[256,256]{1,0:T(8,128)(2,1)} %constant.10.clone.tx_ref, bf16[576,576]{1,0:T(8,128)(2,1)} %constant.11.clone.ty_ref, bf16[384,384]{1,0:T(8,128)(2,1)} %constant.12.clone.tz_ref, ...), custom_call_target="tpu_custom_call" | custom-call | tf_op jit(solution)/shard_map/exchange/pallas_call | solution.py:418
  48.2 0.0 copy-start
  48.2 1.6 %reshape.17 = f32[2,5760]{1,0:T(2,128)} reshape(f32[2,10,576]{2,1,0:T(8,128)} %bitcast.3) | data formatting | bytes 92160 | tf_op jit(solution)/shard_map/reshape | solution.py:455
  49.8 0.0 copy-done
  49.8 0.7 %reshape.18 = f32[2,5760]{1,0:T(2,128)} reshape(f32[2,10,576]{2,1,0:T(8,128)S(1)} %bitcast.2) | data formatting | bytes 92160 | tf_op jit(solution)/shard_map/reshape | solution.py:455
  (1 shorter events, 0.0 us)
Async XLA Ops:
  0.6 0.7 %copy-start.1 = (bf16[2]{0:T(256)(128)(2,1)S(1)}, bf16[2]{0:T(256)(128)(2,1)}, u32[]{:S(2)}) copy-start(bf16[2]{0:T(256)(128)(2,1)} %param.7) | copy-start | bytes 16
  48.2 1.7 %copy-start = (f32[2,16,576]{2,1,0:T(8,128)S(1)}, f32[2,16,576]{2,1,0:T(8,128)}, u32[]{:S(2)}) copy-start(f32[2,16,576]{2,1,0:T(8,128)} %get-tuple-element.5) | copy-start | bytes 221188

commit v2 on v1

v2 whole, which is shorter than its diff:
```python
import functools
import math

import jax
import jax.numpy as jnp
import numpy as np
from jax import lax
from jax.experimental import pallas as pl
from jax.experimental.pallas import tpu as pltpu
from jax.sharding import PartitionSpec as P

NX = 20
NY = 24
NZ = 24
NPTS = NX * NY * NZ
PLANE = NY * NZ
HALVES = 2
HX = NX // HALVES
ROWS = 16
SENT = 12
BATCH = 8
MESH = pl.DeviceIdType.MESH


def hartley_table(length):
    index = np.arange(length, dtype=np.int32)
    product = index[:, None] * index[None, :] % length
    angle = np.float32(2.0 * math.pi / length) * product.astype(np.float32)
    return np.cos(angle) + np.sin(angle)


def signed_square(length):
    index = np.arange(length, dtype=np.int32)
    signed = np.where(index <= length // 2, index, index - length).astype(np.float32)
    return (np.float32(2.0 * math.pi) * signed / np.float32(length)) ** 2


def padded_rows(array):
    halves = array.reshape((HALVES, HX) + array.shape[1:])
    pad = [(0, 0), (0, ROWS - HX)] + [(0, 0)] * (array.ndim - 1)
    return np.pad(halves, pad).reshape((HALVES * ROWS,) + array.shape[1:])


def tables():
    table_x = padded_rows(padded_rows(hartley_table(NX)).T)
    table_x = np.kron(np.eye(BATCH, dtype=np.float32), table_x)
    table_y = np.kron(hartley_table(NY), np.eye(NZ, dtype=np.float32))
    table_z = np.kron(np.eye(16, dtype=np.float32), hartley_table(NZ))
    total = (
        signed_square(NX)[:, None, None]
        + signed_square(NY)[None, :, None]
        + signed_square(NZ)[None, None, :]
    )
    safe = np.where(total > 0, total, 1.0)
    kernel = np.where(total > 0, 1.0 / safe, 0.0) / NPTS
    kernel = padded_rows(kernel.reshape(NX, PLANE).astype(np.float32))
    return (
        jnp.asarray(table_x, jnp.bfloat16),
        jnp.asarray(table_y, jnp.bfloat16),
        jnp.asarray(table_z, jnp.bfloat16),
        jnp.asarray(kernel, jnp.float32),
    )


def column_of(matrix, k):
    if isinstance(k, int):
        return matrix[:, k : k + 1]
    lane = lax.broadcasted_iota(jnp.int32, matrix.shape, 1)
    return jnp.sum(jnp.where(lane == k, matrix, 0.0), axis=1, keepdims=True)


def row_of(matrix, k):
    if isinstance(k, int):
        return matrix[k : k + 1, :]
    line = lax.broadcasted_iota(jnp.int32, matrix.shape, 0)
    return jnp.sum(jnp.where(line == k, matrix, 0.0), axis=0, keepdims=True)


def loop(count, body, carry, most=64):
    if count <= most:
        for k in range(count):
            carry = body(k, carry)
        return carry
    return lax.fori_loop(0, count, body, carry)


def body(
    cols,
    own_ref,
    occ_ref,
    tx_hbm,
    ty_hbm,
    tz_hbm,
    k_hbm,
    pot_ref,
    proj_ref,
    tx_ref,
    ty_ref,
    tz_ref,
    k_ref,
    src,
    part,
    part_in,
    pots,
    rowsum,
    gown,
    gall,
    gmat,
    s_tab,
    s_x,
    r_x,
    s_a,
    s_y,
    s_c,
    r_in,
    s_p,
    r_p,
    s_g,
    r_g,
    t_a,
    t_y,
    t_c,
    t_in,
):
    o = lax.axis_index("orb")
    g = lax.axis_index("grid")
    n_orb = 4 * cols
    n = 2 * n_orb
    r = o // 4
    y = (o % 4) // 2
    c = o % 2
    h = 1 - g
    f32 = jnp.float32
    bf16 = jnp.bfloat16
    o_y = r * 4 + (1 - y) * 2 + c
    o_c = r * 4 + y * 2 + (1 - c)

    loads = [
        pltpu.make_async_copy(a, b, s_tab.at[i])
        for i, (a, b) in enumerate(
            ((tx_hbm, tx_ref), (ty_hbm, ty_ref), (tz_hbm, tz_ref), (k_hbm, k_ref))
        )
    ]
    for load in loads:
        load.start()

    barrier = pltpu.get_barrier_semaphore()

    @pl.loop(1, 2 * n_orb)
    def _(d):
        flat = (o * 2 + g + d) % (2 * n_orb)
        pl.semaphore_signal(
            barrier, inc=1, device_id=(flat // 2, flat % 2), device_id_type=MESH
        )

    own = own_ref[...].astype(f32)
    occ = occ_ref[...].astype(f32)
    for t in range(2):
        lines = [own[t : t + 1, PLANE * x : PLANE * (x + 1)] for x in range(HX)]
        lines.append(jnp.broadcast_to(occ[:, t : t + 1], (1, PLANE)))
        lines.append(jnp.zeros((SENT - HX - 1, PLANE), f32))
        src[r, y, c, g, t] = jnp.concatenate(lines, axis=0).astype(bf16)

    pl.semaphore_wait(barrier, 2 * n_orb - 1)

    def copy(source, target, send, recv, orb, grid):
        return pltpu.make_async_remote_copy(
            src_ref=source,
            dst_ref=target,
            send_sem=send,
            recv_sem=recv,
            device_id=(orb, grid),
            device_id_type=MESH,
        )

    def piece(j, q, u, w):
        half = h if j == 1 else g
        t = h if j == 2 else g
        return src.at[q, u, w, half, t]

    def same(ref, send, recv, orb):
        return copy(ref, ref, send, recv, orb, g)

    def to_column(j, d):
        q = (r + d) % cols
        return same(piece(j, r, y, c), s_a.at[j, q], r_in.at[j, r, y, c], q * 4 + y * 2 + c)

    def to_y(j, q):
        return same(piece(j, q, y, c), s_y.at[j, q], r_in.at[j, q, y, c], o_y)

    def to_core(j, q, u):
        return same(piece(j, q, u, c), s_c.at[j, q, u], r_in.at[j, q, u, c], o_c)

    def arrived(j, q, u, w):
        same(piece(j, q, u, w), s_a.at[j, r], r_in.at[j, q, u, w], o_c).wait_recv()

    own_block = src.at[r, y, c, g]
    cross = copy(own_block, own_block, s_x, r_x, o, h)
    other_block = src.at[r, y, c, h]
    cross_in = copy(other_block, other_block, s_x, r_x, o, h)
    cross.start()

    def send_own(j):
        @pl.loop(1, cols)
        def _(d):
            to_column(j, cols - d).start()

        to_y(j, r).start()
        to_core(j, r, y).start()

    send_own(0)
    cross_in.wait_recv()
    send_own(1)

    def relay_column(j):
        @pl.loop(1, cols)
        def _(d):
            q = (r + d) % cols
            arrived(j, q, y, c)
            to_y(j, q).start()
            to_core(j, q, y).start()

    def relay_y(j):
        @pl.loop(0, cols)
        def _(d):
            q = (r + d) % cols
            arrived(j, q, 1 - y, c)
            to_core(j, q, 1 - y).start()

    def other_core(j, u):
        @pl.loop(0, cols)
        def _(q):
            arrived(j, q, u, 1 - c)

    relay_column(0)
    relay_column(1)
    send_own(2)
    for load in loads:
        load.wait()
    other_core(0, y)
    other_core(1, y)

    tx = tx_ref[...]
    ty = ty_ref[...]
    tz = tz_ref[...]
    cut = tz.shape[0]
    rest = PLANE - cut
    kern = k_ref[...]

    def mm(a, b):
        return jnp.dot(a, b, preferred_element_type=f32)

    def along_z(a):
        return jnp.concatenate([mm(a[:, :cut], tz), mm(a[:, cut:], tz[:rest, :rest])], axis=1)

    per = BATCH // 2
    block = (BATCH, HALVES * ROWS, PLANE)
    flat_block = (BATCH * HALVES * ROWS, PLANE)
    steps = cols // per
    thin = (BATCH * HALVES, SENT, PLANE)

    def whole(a):
        a = a.astype(f32)
        if SENT == ROWS:
            return a
        fill = jnp.zeros((a.shape[0], ROWS - SENT, PLANE), f32)
        return jnp.concatenate([a, fill], axis=1)

    def one_batch(u, step, t, first):
        raw = whole(src[pl.ds(step * per, per), u, :, :, g].reshape(thin)).reshape(block)
        weight = raw[:, HX : HX + 1, :]
        target = whole(src[r, y, c, :, t]).reshape(block[1:])
        density = (raw * target[None]).astype(bf16).reshape(flat_block)
        s = mm(tx, density).astype(bf16)
        s = mm(s, ty).astype(bf16)
        s = along_z(s).reshape(block) * kern[None]
        s = along_z(s.reshape(flat_block).astype(bf16)).astype(bf16)
        s = mm(s, ty).astype(bf16)
        v = mm(tx, s).reshape(block)
        total = jnp.sum(weight * v * raw, axis=0).reshape(HALVES, ROWS, PLANE)[:, :HX]
        if first:
            part[:, t] = -total
        else:
            part[:, t] -= total

    def batches(u, t, first):
        if first:
            one_batch(u, 0, t, True)
        if steps > int(first):

            @pl.loop(int(first), steps)
            def _(k):
                one_batch(u, k, t, False)

    batches(y, 0, True)
    relay_y(0)
    relay_y(1)
    batches(y, 1, True)
    relay_column(2)
    other_core(0, 1 - y)
    other_core(1, 1 - y)
    batches(1 - y, 0, False)

    def swap(t):
        return copy(part.at[h, t], part_in.at[t], s_p.at[t], r_p.at[t], o, h)

    swap(0).start()
    relay_y(2)
    batches(1 - y, 1, False)
    swap(1).start()

    other_core(2, y)
    other_core(2, 1 - y)

    def pot_at(t, q, u, w):
        return pots.at[q, u, w, t]

    def pot_column(t, d):
        q = (r + d) % cols
        return same(pot_at(t, r, y, c), t_a.at[t, q], t_in.at[t, r, y, c], q * 4 + y * 2 + c)

    def pot_y(t, q):
        return same(pot_at(t, q, y, c), t_y.at[t, q], t_in.at[t, q, y, c], o_y)

    def pot_core(t, q, u):
        return same(pot_at(t, q, u, c), t_c.at[t, q, u], t_in.at[t, q, u, c], o_c)

    def pot_arrived(t, q, u, w):
        same(pot_at(t, q, u, w), t_a.at[t, r], t_in.at[t, q, u, w], o_c).wait_recv()

    def send_pots(t):
        @pl.loop(1, cols)
        def _(d):
            pot_column(t, cols - d).start()

        pot_y(t, r).start()
        pot_core(t, r, y).start()

    def gram_rows(t, value):
        @pl.loop(0, cols)
        def _(q):
            rows = src[q, :, :, g].reshape(8, SENT, PLANE).astype(f32)[:, :HX]
            rowsum[t, pl.ds(pl.multiple_of(q * 8, 8), 8), :] = jnp.sum(rows * value[None], axis=1)

        ones = jnp.ones((8, PLANE), f32)
        sums = lax.dot_general(
            ones,
            rowsum[t],
            (((1,), (1,)), ((), ())),
            precision=lax.Precision.HIGHEST,
            preferred_element_type=f32,
        )
        gown[t : t + 1, :] = sums[0:1]

    def finish(t):
        swap(t).wait_recv()
        value = part[g, t] + part_in[t]
        pots[r, y, c, t] = value
        return value

    value0 = finish(0)
    send_pots(0)
    gram_rows(0, value0)
    value1 = finish(1)
    gram_rows(1, value1)
    gall[g, o] = gown[...]

    def gram_to(d):
        flat = (o * 2 + g + d) % (2 * n_orb)
        return copy(gown, gall.at[g, o], s_g.at[d], r_g.at[g, o], flat // 2, flat % 2)

    @pl.loop(1, 2 * n_orb)
    def _(d):
        gram_to(d).start()

    send_pots(1)

    def write(ref, t, value):
        for x in range(0, HX, 2):
            pair = jnp.concatenate([value[x : x + 1], value[x + 1 : x + 2]], axis=1)
            ref[t : t + 1, PLANE * x : PLANE * (x + 2)] = pair

    write(pot_ref, 0, value0)
    write(pot_ref, 1, value1)

    def pot_relay_column(t):
        @pl.loop(1, cols)
        def _(d):
            q = (r + d) % cols
            pot_arrived(t, q, y, c)
            pot_y(t, q).start()
            pot_core(t, q, y).start()

    def pot_relay_y(t):
        @pl.loop(0, cols)
        def _(d):
            q = (r + d) % cols
            pot_arrived(t, q, 1 - y, c)
            pot_core(t, q, 1 - y).start()

    pot_relay_column(0)

    @pl.loop(1, 2 * n_orb)
    def _(d):
        flat = (o * 2 + g + d) % (2 * n_orb)
        there = gall.at[flat % 2, flat // 2]
        copy(there, there, s_g.at[0], r_g.at[flat % 2, flat // 2], o_c, g).wait_recv()

    pot_relay_column(1)
    pot_relay_y(0)

    def assemble(k, carry):
        pairs = [gall[0, 4 * k + j] + gall[1, 4 * k + j] for j in range(4)]
        start = 8 * k if isinstance(k, int) else pl.multiple_of(8 * k, 8)
        gmat[pl.ds(start, 8), :] = jnp.concatenate(pairs, axis=0)
        return carry

    loop(cols, assemble, 0, 16)
    gram = gmat[...]
    sym = (gram + gram.T) * f32(-0.5 / NPTS)
    row_id = lax.broadcasted_iota(jnp.int32, (n, n), 0)
    eye = (row_id == lax.broadcasted_iota(jnp.int32, (n, n), 1)).astype(f32)
    below = lax.broadcasted_iota(jnp.int32, (n, 1), 0)

    def eliminate(k, pair):
        left, right = pair
        row_l = row_of(left, k)
        scale = 1.0 / column_of(row_l, k)
        factor = jnp.where(below > k, column_of(left, k) * scale, 0.0)
        return left - factor * row_l, right - factor * row_of(right, k)

    left, right = loop(n, eliminate, (sym, eye))
    diag = jnp.sum(left * eye, axis=1, keepdims=True)
    inverse = right * (1.0 / jnp.sqrt(diag))
    a0, a1 = row_of(inverse, 2 * o), row_of(inverse, 2 * o + 1)

    pot_relay_y(1)

    @pl.loop(0, cols)
    def _(q):
        for u in range(2):
            for t in range(2):
                pot_arrived(t, q, u, 1 - c)

    def add(k, sums):
        p0, p1 = sums
        if isinstance(k, int):
            value = pots[k // 8, (k % 8) // 4, (k % 4) // 2, k % 2]
        else:
            value = pots[k // 8, lax.rem(k, 8) // 4, lax.rem(k, 4) // 2, lax.rem(k, 2)]
        return p0 + column_of(a0, k) * value, p1 + column_of(a1, k) * value

    zero = jnp.zeros((HX, PLANE), f32)
    p0, p1 = loop(n, add, (zero, zero))
    write(proj_ref, 0, p0)
    write(proj_ref, 1, p1)

    cross.wait_send()
    for t in range(2):
        swap(t).wait_send()

    @pl.loop(1, cols)
    def _(d):
        for j in range(3):
            to_column(j, d).wait_send()
        for t in range(2):
            pot_column(t, d).wait_send()

    @pl.loop(0, cols)
    def _(q):
        for j in range(3):
            to_y(j, q).wait_send()
            for u in range(2):
                to_core(j, q, u).wait_send()
        for t in range(2):
            pot_y(t, q).wait_send()
            for u in range(2):
                pot_core(t, q, u).wait_send()

    @pl.loop(1, 2 * n_orb)
    def _(d):
        gram_to(d).wait_send()


def on_device(orbitals, occupation):
    n_orb = lax.axis_size("orb")
    cols = n_orb // 4
    n = 2 * n_orb
    consts = tables()
    f32 = jnp.float32
    bf16 = jnp.bfloat16
    dma = pltpu.SemaphoreType.DMA
    vmem = pl.BlockSpec(memory_space=pltpu.VMEM)
    full = jax.ShapeDtypeStruct(orbitals.shape, f32)
    return pl.pallas_call(
        functools.partial(body, cols),
        out_shape=(full, full),
        in_specs=[vmem] * 2 + [pl.BlockSpec(memory_space=pl.ANY)] * 4,
        out_specs=(vmem, vmem),
        scratch_shapes=[
            *[pltpu.VMEM(a.shape, a.dtype) for a in consts],
            pltpu.VMEM((cols, 2, 2, 2, 2, SENT, PLANE), bf16),
            pltpu.VMEM((2, 2, HX, PLANE), f32),
            pltpu.VMEM((2, HX, PLANE), f32),
            pltpu.VMEM((cols, 2, 2, 2, HX, PLANE), f32),
            pltpu.VMEM((2, n, PLANE), f32),
            pltpu.VMEM((2, n), f32),
            pltpu.VMEM((2, n_orb, 2, n), f32),
            pltpu.VMEM((n, n), f32),
            dma((4,)),
            dma,
            dma,
            dma((3, cols)),
            dma((3, cols)),
            dma((3, cols, 2)),
            dma((3, cols, 2, 2)),
            dma((2,)),
            dma((2,)),
            dma((2 * n_orb,)),
            dma((2, n_orb)),
            dma((2, cols)),
            dma((2, cols)),
            dma((2, cols, 2)),
            dma((2, cols, 2, 2)),
        ],
        compiler_params=pltpu.CompilerParams(
            collective_id=0, has_side_effects=True, vmem_limit_bytes=60 * 1024 * 1024
        ),
        name="exchange",
    )(orbitals, occupation[None], *consts)


def solution(mesh):
    return jax.shard_map(
        on_device,
        mesh=mesh,
        in_specs=(P("orb", "grid"), P("orb")),
        out_specs=(P("orb", "grid"), P("orb", "grid")),
        check_vma=False,
    )
```

time: 50.8 us -> 43.7 us (0.86)
  Pallas kernels: 45.2 us -> 40.4 us
  local copies, waits for them, and re-layouts: 3.93 us -> 2.05 us
  other arithmetic: 0.69 us -> 0 us
    pallas_call x1, Pallas kernels: 45.2 us -> 40.4 us  [on_device(): pl.pallas_call(functools.partial(body, cols), out_shape=(full, full), in_...]
    reshape x3 -> x0, local copies, waits for them, and re-layouts: 3.2 us -> none  [the longest x2 2.36 us: flat(): return a[:, :HX, :].reshape(2, HX * PLANE)]
    unnamed x4, local copies, waits for them, and re-layouts: 0.58 us -> 2.05 us
    concatenate x1 -> x0, other arithmetic: 0.69 us -> none  [on_device(): own = jnp.concatenate([own, weight, fill], axis=1)]
where the time goes in v2:
time: 43.7 us; the launch traced here: 43.1 us
  Pallas kernels  40.4 us (92%)
  local copies, waits for them, and re-layouts  2.05 us (5%)
  between operations  0.65 us (1%)
    pallas_call x1, Pallas kernels, on_device(): pl.pallas_call(functools.partial(body, cols), out_shape=(full, full), in_...  40.4 us
    unnamed x4, local copies, waits for them, and re-layouts  2.05 us

profile of v2, /device:TPU:0, one launch (start us, length us, event | category | flops | bytes accessed | tf_op | source)
XLA Modules:
  0.0 43.1 jit_solution(16618321353594012737)
XLA Ops:
  0.6 40.4 %exchange.1 = (f32[2,5760]{1,0:T(2,128)}, f32[2,5760]{1,0:T(2,128)}) custom-call(bf16[2,5760]{1,0:T(2,128)(2,1)} %own_ref.1, bf16[1,2]{1,0:T(2,128)(2,1)} %bitcast.1, bf16[256,256]{1,0:T(8,128)(2,1)} %constant.8.clone.tx_hbm, bf16[576,576]{1,0:T(8,128)(2,1)} %constant.9.clone.ty_hbm, bf16[384,384]{1,0:T(8,128)(2,1)} %constant.10.clone.tz_hbm, ...), custom_call_target="tpu_custom_call" | custom-call | tf_op jit(solution)/shard_map/exchange/pallas_call | solution.py:495
  41.0 0.0 copy-start
  41.0 1.4 %copy.10 = f32[2,5760]{1,0:T(2,128)} copy(f32[2,5760]{1,0:T(2,128)} %get-tuple-element.4) | data formatting | bytes 92160
  42.5 0.0 copy-done
  42.5 0.6 %copy.11 = f32[2,5760]{1,0:T(2,128)} copy(f32[2,5760]{1,0:T(2,128)S(1)} %copy-done) | data formatting | bytes 92160
Async XLA Ops:
  41.0 1.4 %copy-start = (f32[2,5760]{1,0:T(2,128)S(1)}, f32[2,5760]{1,0:T(2,128)}, u32[]{:S(2)}) copy-start(f32[2,5760]{1,0:T(2,128)} %get-tuple-element.5) | copy-start | bytes 138244

commit v3 on v2

--- a/solution.py
+++ b/solution.py
@@ -18,6 +18,7 @@
 HX = NX // HALVES
 ROWS = 16
 SENT = 12
+LANES = 128
 BATCH = 8
 MESH = pl.DeviceIdType.MESH
 
@@ -146,12 +147,16 @@
 
     barrier = pltpu.get_barrier_semaphore()
 
-    @pl.loop(1, 2 * n_orb)
+    def greet(orb, grid):
+        pl.semaphore_signal(barrier, inc=1, device_id=(orb, grid), device_id_type=MESH)
+
+    @pl.loop(1, cols)
     def _(d):
-        flat = (o * 2 + g + d) % (2 * n_orb)
-        pl.semaphore_signal(
-            barrier, inc=1, device_id=(flat // 2, flat % 2), device_id_type=MESH
-        )
+        greet((r + d) % cols * 4 + y * 2 + c, g)
+
+    greet(o, h)
+    greet(o_y, g)
+    greet(o_c, g)
 
     own = own_ref[...].astype(f32)
     occ = occ_ref[...].astype(f32)
@@ -161,7 +166,7 @@
         lines.append(jnp.zeros((SENT - HX - 1, PLANE), f32))
         src[r, y, c, g, t] = jnp.concatenate(lines, axis=0).astype(bf16)
 
-    pl.semaphore_wait(barrier, 2 * n_orb - 1)
+    pl.semaphore_wait(barrier, cols + 2)
 
     def copy(source, target, send, recv, orb, grid):
         return pltpu.make_async_remote_copy(
@@ -305,12 +310,10 @@
         return copy(part.at[h, t], part_in.at[t], s_p.at[t], r_p.at[t], o, h)
 
     swap(0).start()
-    relay_y(2)
     batches(1 - y, 1, False)
     swap(1).start()
 
-    other_core(2, y)
-    other_core(2, 1 - y)
+    relay_y(2)
 
     def pot_at(t, q, u, w):
         return pots.at[q, u, w, t]
@@ -340,9 +343,17 @@
         @pl.loop(0, cols)
         def _(q):
             rows = src[q, :, :, g].reshape(8, SENT, PLANE).astype(f32)[:, :HX]
-            rowsum[t, pl.ds(pl.multiple_of(q * 8, 8), 8), :] = jnp.sum(rows * value[None], axis=1)
-
-        ones = jnp.ones((8, PLANE), f32)
+            sums = jnp.sum(rows * value[None], axis=1)
+            fold = sums[:, :LANES]
+            for k in range(LANES, PLANE - LANES + 1, LANES):
+                fold += sums[:, k : k + LANES]
+            tail = PLANE % LANES
+            if tail:
+                last = jnp.zeros((8, LANES - tail), f32)
+                fold += jnp.concatenate([sums[:, PLANE - tail :], last], axis=1)
+            rowsum[t, pl.ds(pl.multiple_of(q * 8, 8), 8), :] = fold
+
+        ones = jnp.ones((8, LANES), f32)
         sums = lax.dot_general(
             ones,
             rowsum[t],
@@ -360,6 +371,8 @@
 
     value0 = finish(0)
     send_pots(0)
+    other_core(2, y)
+    other_core(2, 1 - y)
     gram_rows(0, value0)
     value1 = finish(1)
     gram_rows(1, value1)
@@ -399,15 +412,30 @@
             pot_core(t, q, 1 - y).start()
 
     pot_relay_column(0)
+    pot_relay_column(1)
+    pot_relay_y(0)
+
+    cross.wait_send()
+    for t in range(2):
+        swap(t).wait_send()
+
+    @pl.loop(1, cols)
+    def _(d):
+        for j in range(3):
+            to_column(j, d).wait_send()
+
+    @pl.loop(0, cols)
+    def _(q):
+        for j in range(3):
+            to_y(j, q).wait_send()
+            for u in range(2):
+                to_core(j, q, u).wait_send()
 
     @pl.loop(1, 2 * n_orb)
     def _(d):
         flat = (o * 2 + g + d) % (2 * n_orb)
         there = gall.at[flat % 2, flat // 2]
         copy(there, there, s_g.at[0], r_g.at[flat % 2, flat // 2], o_c, g).wait_recv()
-
-    pot_relay_column(1)
-    pot_relay_y(0)
 
     def assemble(k, carry):
         pairs = [gall[0, 4 * k + j] + gall[1, 4 * k + j] for j in range(4)]
@@ -429,12 +457,19 @@
         factor = jnp.where(below > k, column_of(left, k) * scale, 0.0)
         return left - factor * row_l, right - factor * row_of(right, k)
 
-    left, right = loop(n, eliminate, (sym, eye))
+    early = n * 3 // 4
+    if n <= 64:
+        pair = loop(early, eliminate, (sym, eye))
+        pot_relay_y(1)
+        for k in range(early, n):
+            pair = eliminate(k, pair)
+        left, right = pair
+    else:
+        pot_relay_y(1)
+        left, right = loop(n, eliminate, (sym, eye))
     diag = jnp.sum(left * eye, axis=1, keepdims=True)
     inverse = right * (1.0 / jnp.sqrt(diag))
     a0, a1 = row_of(inverse, 2 * o), row_of(inverse, 2 * o + 1)
-
-    pot_relay_y(1)
 
     @pl.loop(0, cols)
     def _(q):
@@ -455,23 +490,13 @@
     write(proj_ref, 0, p0)
     write(proj_ref, 1, p1)
 
-    cross.wait_send()
-    for t in range(2):
-        swap(t).wait_send()
-
     @pl.loop(1, cols)
     def _(d):
-        for j in range(3):
-            to_column(j, d).wait_send()
         for t in range(2):
             pot_column(t, d).wait_send()
 
     @pl.loop(0, cols)
     def _(q):
-        for j in range(3):
-            to_y(j, q).wait_send()
-            for u in range(2):
-                to_core(j, q, u).wait_send()
         for t in range(2):
             pot_y(t, q).wait_send()
             for u in range(2):
@@ -503,7 +528,7 @@
             pltpu.VMEM((2, 2, HX, PLANE), f32),
             pltpu.VMEM((2, HX, PLANE), f32),
             pltpu.VMEM((cols, 2, 2, 2, HX, PLANE), f32),
-            pltpu.VMEM((2, n, PLANE), f32),
+            pltpu.VMEM((2, n, LANES), f32),
             pltpu.VMEM((2, n), f32),
             pltpu.VMEM((2, n_orb, 2, n), f32),
             pltpu.VMEM((n, n), f32),

time: 43.7 us -> 43.5 us (level)
  the two profiles are of different devices: /device:TPU:0 before, /device:TPU:3 now
where the time goes in v3:
time: 43.5 us; the launch traced here: 43.2 us
  Pallas kernels  40.5 us (93%)
  local copies, waits for them, and re-layouts  2.05 us (5%)
  between operations  0.65 us (1%)
    pallas_call x1, Pallas kernels, on_device(): pl.pallas_call(functools.partial(body, cols), out_shape=(full, full), in_...  40.5 us
    unnamed x4, local copies, waits for them, and re-layouts  2.05 us

profile of v3, /device:TPU:3, one launch (start us, length us, event | category | flops | bytes accessed | tf_op | source)
XLA Modules:
  0.0 43.2 jit_solution(7368608095410038824)
XLA Ops:
  0.6 40.5 %exchange.1 = (f32[2,5760]{1,0:T(2,128)}, f32[2,5760]{1,0:T(2,128)}) custom-call(bf16[2,5760]{1,0:T(2,128)(2,1)} %own_ref.1, bf16[1,2]{1,0:T(2,128)(2,1)} %bitcast.1, bf16[256,256]{1,0:T(8,128)(2,1)} %constant.8.clone.tx_hbm, bf16[576,576]{1,0:T(8,128)(2,1)} %constant.9.clone.ty_hbm, bf16[384,384]{1,0:T(8,128)(2,1)} %constant.10.clone.tz_hbm, ...), custom_call_target="tpu_custom_call" | custom-call | tf_op jit(solution)/shard_map/exchange/pallas_call | solution.py:520
  41.2 0.0 copy-start
  41.2 1.4 %copy.10 = f32[2,5760]{1,0:T(2,128)} copy(f32[2,5760]{1,0:T(2,128)} %get-tuple-element.4) | data formatting | bytes 92160
  42.6 0.0 copy-done
  42.6 0.6 %copy.11 = f32[2,5760]{1,0:T(2,128)} copy(f32[2,5760]{1,0:T(2,128)S(1)} %copy-done) | data formatting | bytes 92160
Async XLA Ops:
  41.2 1.4 %copy-start = (f32[2,5760]{1,0:T(2,128)S(1)}, f32[2,5760]{1,0:T(2,128)}, u32[]{:S(2)}) copy-start(f32[2,5760]{1,0:T(2,128)} %get-tuple-element.5) | copy-start | bytes 138244

commit v4 on v3

--- a/solution.py
+++ b/solution.py
@@ -16,8 +16,9 @@
 PLANE = NY * NZ
 HALVES = 2
 HX = NX // HALVES
-ROWS = 16
-SENT = 12
+TILE = 8
+EDGE = HX - TILE
+ROWS = 3 * TILE
 LANES = 128
 BATCH = 8
 MESH = pl.DeviceIdType.MESH
@@ -37,9 +38,10 @@
 
 
 def padded_rows(array):
-    halves = array.reshape((HALVES, HX) + array.shape[1:])
-    pad = [(0, 0), (0, ROWS - HX)] + [(0, 0)] * (array.ndim - 1)
-    return np.pad(halves, pad).reshape((HALVES * ROWS,) + array.shape[1:])
+    zero = np.zeros((TILE - 2 * EDGE,) + array.shape[1:], array.dtype)
+    first, second = array[:HX], array[HX:]
+    parts = [first[:TILE], first[TILE:], second[TILE:], zero, second[:TILE]]
+    return np.concatenate(parts, axis=0)
 
 
 def tables():
@@ -103,6 +105,9 @@
     part,
     part_in,
     pots,
+    pedge,
+    edge_out,
+    edge_in,
     rowsum,
     gown,
     gall,
@@ -160,11 +165,13 @@
 
     own = own_ref[...].astype(f32)
     occ = occ_ref[...].astype(f32)
+    own_edges = []
     for t in range(2):
         lines = [own[t : t + 1, PLANE * x : PLANE * (x + 1)] for x in range(HX)]
-        lines.append(jnp.broadcast_to(occ[:, t : t + 1], (1, PLANE)))
-        lines.append(jnp.zeros((SENT - HX - 1, PLANE), f32))
-        src[r, y, c, g, t] = jnp.concatenate(lines, axis=0).astype(bf16)
+        src[r, y, c, t, 2 * g] = jnp.concatenate(lines[:TILE], axis=0).astype(bf16)
+        own_edges += lines[TILE:]
+    own_edges = jnp.concatenate(own_edges + [jnp.zeros((2 * EDGE, PLANE), f32)], axis=0)
+    edge_out[...] = own_edges.astype(bf16)
 
     pl.semaphore_wait(barrier, cols + 2)
 
@@ -179,9 +186,11 @@
         )
 
     def piece(j, q, u, w):
-        half = h if j == 1 else g
-        t = h if j == 2 else g
-        return src.at[q, u, w, half, t]
+        if j == 0:
+            return src.at[q, u, w, g, 2 * g]
+        if j == 1:
+            return src.at[q, u, w, g, pl.ds(h, 2)]
+        return src.at[q, u, w, h, pl.ds(g, 2)]
 
     def same(ref, send, recv, orb):
         return copy(ref, ref, send, recv, orb, g)
@@ -199,11 +208,13 @@
     def arrived(j, q, u, w):
         same(piece(j, q, u, w), s_a.at[j, r], r_in.at[j, q, u, w], o_c).wait_recv()
 
-    own_block = src.at[r, y, c, g]
-    cross = copy(own_block, own_block, s_x, r_x, o, h)
-    other_block = src.at[r, y, c, h]
-    cross_in = copy(other_block, other_block, s_x, r_x, o, h)
-    cross.start()
+    def crossing(half):
+        tile = src.at[r, y, c, :, 2 * half]
+        return copy(tile, tile, s_x.at[0], r_x.at[0], o, h)
+
+    crosses = (crossing(g), copy(edge_out, edge_in, s_x.at[1], r_x.at[1], o, h))
+    for cross in crosses:
+        cross.start()
 
     def send_own(j):
         @pl.loop(1, cols)
@@ -214,7 +225,19 @@
         to_core(j, r, y).start()
 
     send_own(0)
-    cross_in.wait_recv()
+    crossing(h).wait_recv()
+    crosses[1].wait_recv()
+    second_half = g.astype(f32)
+    first_half = 1.0 - second_half
+    edges = edge_in[...].astype(f32)
+    low = own_edges * first_half + edges * second_half
+    high = edges * first_half + own_edges * second_half
+    for t in range(2):
+        own_lines = slice(EDGE * t, EDGE * (t + 1))
+        lines = [low[own_lines], high[own_lines]]
+        lines.append(jnp.broadcast_to(occ[:, t : t + 1], (1, PLANE)))
+        lines.append(jnp.zeros((TILE - 2 * EDGE - 1, PLANE), f32))
+        src[r, y, c, t, 1] = jnp.concatenate(lines, axis=0).astype(bf16)
     send_own(1)
 
     def relay_column(j):
@@ -259,34 +282,27 @@
         return jnp.concatenate([mm(a[:, :cut], tz), mm(a[:, cut:], tz[:rest, :rest])], axis=1)
 
     per = BATCH // 2
-    block = (BATCH, HALVES * ROWS, PLANE)
-    flat_block = (BATCH * HALVES * ROWS, PLANE)
+    block = (BATCH, ROWS, PLANE)
+    flat_block = (BATCH * ROWS, PLANE)
     steps = cols // per
-    thin = (BATCH * HALVES, SENT, PLANE)
-
-    def whole(a):
-        a = a.astype(f32)
-        if SENT == ROWS:
-            return a
-        fill = jnp.zeros((a.shape[0], ROWS - SENT, PLANE), f32)
-        return jnp.concatenate([a, fill], axis=1)
 
     def one_batch(u, step, t, first):
-        raw = whole(src[pl.ds(step * per, per), u, :, :, g].reshape(thin)).reshape(block)
-        weight = raw[:, HX : HX + 1, :]
-        target = whole(src[r, y, c, :, t]).reshape(block[1:])
-        density = (raw * target[None]).astype(bf16).reshape(flat_block)
+        raw = src[pl.ds(step * per, per), u, :, g].reshape(BATCH * 3, TILE, PLANE)
+        raw = raw.astype(f32).reshape(block)
+        weight = raw[:, TILE + 2 * EDGE : TILE + 2 * EDGE + 1, :]
+        target = src[r, y, c, t].astype(f32).reshape(block[1:])
+        density = (raw * target[None]).reshape(flat_block).astype(bf16)
         s = mm(tx, density).astype(bf16)
         s = mm(s, ty).astype(bf16)
         s = along_z(s).reshape(block) * kern[None]
         s = along_z(s.reshape(flat_block).astype(bf16)).astype(bf16)
         s = mm(s, ty).astype(bf16)
         v = mm(tx, s).reshape(block)
-        total = jnp.sum(weight * v * raw, axis=0).reshape(HALVES, ROWS, PLANE)[:, :HX]
+        total = jnp.sum(weight * v * raw, axis=0).reshape(3, TILE, PLANE)
         if first:
-            part[:, t] = -total
+            part[t] = -total
         else:
-            part[:, t] -= total
+            part[t] -= total
 
     def batches(u, t, first):
         if first:
@@ -307,7 +323,7 @@
     batches(1 - y, 0, False)
 
     def swap(t):
-        return copy(part.at[h, t], part_in.at[t], s_p.at[t], r_p.at[t], o, h)
+        return copy(part.at[t, pl.ds(h, 2)], part_in.at[t], s_p.at[t], r_p.at[t], o, h)
 
     swap(0).start()
     batches(1 - y, 1, False)
@@ -316,7 +332,7 @@
     relay_y(2)
 
     def pot_at(t, q, u, w):
-        return pots.at[q, u, w, t]
+        return pedge.at[q, u, w] if t == 2 else pots.at[q, u, w, t]
 
     def pot_column(t, d):
         q = (r + d) % cols
@@ -342,8 +358,9 @@
     def gram_rows(t, value):
         @pl.loop(0, cols)
         def _(q):
-            rows = src[q, :, :, g].reshape(8, SENT, PLANE).astype(f32)[:, :HX]
-            sums = jnp.sum(rows * value[None], axis=1)
+            rows = src[q, :, :, :, 2 * g].reshape(8, TILE, PLANE).astype(f32)
+            ends = src[q, :, :, :, 1].reshape(8, TILE, PLANE).astype(f32)
+            sums = jnp.sum(rows * value[0][None] + ends * value[2][None], axis=1)
             fold = sums[:, :LANES]
             for k in range(LANES, PLANE - LANES + 1, LANES):
                 fold += sums[:, k : k + LANES]
@@ -365,9 +382,12 @@
 
     def finish(t):
         swap(t).wait_recv()
-        value = part[g, t] + part_in[t]
-        pots[r, y, c, t] = value
-        return value
+        tile = part[t, 2 * g] + part_in[t, g]
+        pots[r, y, c, t] = tile
+        rest = part[t, 1] + part_in[t, h]
+        edge = rest[:EDGE] * first_half + rest[EDGE : 2 * EDGE] * second_half
+        line = lax.broadcasted_iota(jnp.int32, (TILE, PLANE), 0)
+        return tile, edge, jnp.where(line // EDGE == g, rest, 0.0)
 
     value0 = finish(0)
     send_pots(0)
@@ -386,15 +406,17 @@
     def _(d):
         gram_to(d).start()
 
+    pedge[r, y, c] = jnp.concatenate([value0[1], value1[1]], axis=0)
     send_pots(1)
+    send_pots(2)
 
     def write(ref, t, value):
         for x in range(0, HX, 2):
             pair = jnp.concatenate([value[x : x + 1], value[x + 1 : x + 2]], axis=1)
             ref[t : t + 1, PLANE * x : PLANE * (x + 2)] = pair
 
-    write(pot_ref, 0, value0)
-    write(pot_ref, 1, value1)
+    write(pot_ref, 0, jnp.concatenate(value0[:2], axis=0))
+    write(pot_ref, 1, jnp.concatenate(value1[:2], axis=0))
 
     def pot_relay_column(t):
         @pl.loop(1, cols)
@@ -413,9 +435,11 @@
 
     pot_relay_column(0)
     pot_relay_column(1)
+    pot_relay_column(2)
     pot_relay_y(0)
 
-    cross.wait_send()
+    for cross in crosses:
+        cross.wait_send()
     for t in range(2):
         swap(t).wait_send()
 
@@ -461,11 +485,13 @@
     if n <= 64:
         pair = loop(early, eliminate, (sym, eye))
         pot_relay_y(1)
+        pot_relay_y(2)
         for k in range(early, n):
             pair = eliminate(k, pair)
         left, right = pair
     else:
         pot_relay_y(1)
+        pot_relay_y(2)
         left, right = loop(n, eliminate, (sym, eye))
     diag = jnp.sum(left * eye, axis=1, keepdims=True)
     inverse = right * (1.0 / jnp.sqrt(diag))
@@ -474,30 +500,37 @@
     @pl.loop(0, cols)
     def _(q):
         for u in range(2):
+            for t in range(3):
+                pot_arrived(t, q, u, 1 - c)
+
+    def add(k, sums):
+        where = (k // 4, k % 4 // 2, k % 2)
+        if not isinstance(k, int):
+            where = (k // 4, lax.rem(k, 4) // 2, lax.rem(k, 2))
+        edge = pedge[where]
+        tiles = [pots[where + (t,)] for t in range(2)]
+        ends = [edge[EDGE * t : EDGE * (t + 1)] for t in range(2)]
+        new = []
+        for a, (tile, end) in zip((a0, a1), sums):
             for t in range(2):
-                pot_arrived(t, q, u, 1 - c)
-
-    def add(k, sums):
-        p0, p1 = sums
-        if isinstance(k, int):
-            value = pots[k // 8, (k % 8) // 4, (k % 4) // 2, k % 2]
-        else:
-            value = pots[k // 8, lax.rem(k, 8) // 4, lax.rem(k, 4) // 2, lax.rem(k, 2)]
-        return p0 + column_of(a0, k) * value, p1 + column_of(a1, k) * value
-
-    zero = jnp.zeros((HX, PLANE), f32)
-    p0, p1 = loop(n, add, (zero, zero))
-    write(proj_ref, 0, p0)
-    write(proj_ref, 1, p1)
+                factor = column_of(a, 2 * k + t)
+                tile, end = tile + factor * tiles[t], end + factor * ends[t]
+            new.append((tile, end))
+        return tuple(new)
+
+    zero = (jnp.zeros((TILE, PLANE), f32), jnp.zeros((EDGE, PLANE), f32))
+    proj = loop(n_orb, add, (zero, zero))
+    for t in range(2):
+        write(proj_ref, t, jnp.concatenate(proj[t], axis=0))
 
     @pl.loop(1, cols)
     def _(d):
-        for t in range(2):
+        for t in range(3):
             pot_column(t, d).wait_send()
 
     @pl.loop(0, cols)
     def _(q):
-        for t in range(2):
+        for t in range(3):
             pot_y(t, q).wait_send()
             for u in range(2):
                 pot_core(t, q, u).wait_send()
@@ -524,17 +557,20 @@
         out_specs=(vmem, vmem),
         scratch_shapes=[
             *[pltpu.VMEM(a.shape, a.dtype) for a in consts],
-            pltpu.VMEM((cols, 2, 2, 2, 2, SENT, PLANE), bf16),
-            pltpu.VMEM((2, 2, HX, PLANE), f32),
-            pltpu.VMEM((2, HX, PLANE), f32),
-            pltpu.VMEM((cols, 2, 2, 2, HX, PLANE), f32),
+            pltpu.VMEM((cols, 2, 2, 2, 3, TILE, PLANE), bf16),
+            pltpu.VMEM((2, 3, TILE, PLANE), f32),
+            pltpu.VMEM((2, 2, TILE, PLANE), f32),
+            pltpu.VMEM((cols, 2, 2, 2, TILE, PLANE), f32),
+            pltpu.VMEM((cols, 2, 2, 2 * EDGE, PLANE), f32),
+            pltpu.VMEM((TILE, PLANE), bf16),
+            pltpu.VMEM((TILE, PLANE), bf16),
             pltpu.VMEM((2, n, LANES), f32),
             pltpu.VMEM((2, n), f32),
             pltpu.VMEM((2, n_orb, 2, n), f32),
             pltpu.VMEM((n, n), f32),
             dma((4,)),
-            dma,
-            dma,
+            dma((2,)),
+            dma((2,)),
             dma((3, cols)),
             dma((3, cols)),
             dma((3, cols, 2)),
@@ -543,10 +579,10 @@
             dma((2,)),
             dma((2 * n_orb,)),
             dma((2, n_orb)),
-            dma((2, cols)),
-            dma((2, cols)),
-            dma((2, cols, 2)),
-            dma((2, cols, 2, 2)),
+            dma((3, cols)),
+            dma((3, cols)),
+            dma((3, cols, 2)),
+            dma((3, cols, 2, 2)),
         ],
         compiler_params=pltpu.CompilerParams(
             collective_id=0, has_side_effects=True, vmem_limit_bytes=60 * 1024 * 1024

time: 43.5 us -> 39.5 us (0.908)
  the two profiles are of different devices: /device:TPU:3 before, /device:TPU:0 now
where the time goes in v4:
time: 39.5 us; the launch traced here: 39.2 us
  Pallas kernels  36.5 us (92%)
  local copies, waits for them, and re-layouts  2.05 us (5%)
  between operations  0.65 us (2%)
    pallas_call x1, Pallas kernels, on_device(): pl.pallas_call(functools.partial(body, cols), out_shape=(full, full), in_...  36.5 us
    unnamed x4, local copies, waits for them, and re-layouts  2.05 us

profile of v4, /device:TPU:0, one launch (start us, length us, event | category | flops | bytes accessed | tf_op | source)
XLA Modules:
  0.0 39.2 jit_solution(4398682433646897546)
XLA Ops:
  0.6 36.5 %exchange.1 = (f32[2,5760]{1,0:T(2,128)}, f32[2,5760]{1,0:T(2,128)}) custom-call(bf16[2,5760]{1,0:T(2,128)(2,1)} %own_ref.1, bf16[1,2]{1,0:T(2,128)(2,1)} %bitcast.1, bf16[192,192]{1,0:T(8,128)(2,1)} %constant.8.clone.tx_hbm, bf16[576,576]{1,0:T(8,128)(2,1)} %constant.9.clone.ty_hbm, bf16[384,384]{1,0:T(8,128)(2,1)} %constant.10.clone.tz_hbm, ...), custom_call_target="tpu_custom_call" | custom-call | tf_op jit(solution)/shard_map/exchange/pallas_call | solution.py:553
  37.1 0.0 copy-start
  37.2 1.4 %copy.10 = f32[2,5760]{1,0:T(2,128)} copy(f32[2,5760]{1,0:T(2,128)} %get-tuple-element.4) | data formatting | bytes 92160
  38.6 0.0 copy-done
  38.6 0.6 %copy.11 = f32[2,5760]{1,0:T(2,128)} copy(f32[2,5760]{1,0:T(2,128)S(1)} %copy-done) | data formatting | bytes 92160
Async XLA Ops:
  37.1 1.4 %copy-start = (f32[2,5760]{1,0:T(2,128)S(1)}, f32[2,5760]{1,0:T(2,128)}, u32[]{:S(2)}) copy-start(f32[2,5760]{1,0:T(2,128)} %get-tuple-element.5) | copy-start | bytes 138244

commit v5 on v4

--- a/solution.py
+++ b/solution.py
@@ -95,8 +95,11 @@
     ty_hbm,
     tz_hbm,
     k_hbm,
+    pot_out,
+    proj_out,
     pot_ref,
     proj_ref,
+    s_o,
     tx_ref,
     ty_ref,
     tz_ref,
@@ -118,7 +121,9 @@
     s_a,
     s_y,
     s_c,
-    r_in,
+    r_col,
+    r_y,
+    r_core,
     s_p,
     r_p,
     s_g,
@@ -126,7 +131,9 @@
     t_a,
     t_y,
     t_c,
-    t_in,
+    t_col,
+    t_yin,
+    t_core,
 ):
     o = lax.axis_index("orb")
     g = lax.axis_index("grid")
@@ -197,16 +204,20 @@
 
     def to_column(j, d):
         q = (r + d) % cols
-        return same(piece(j, r, y, c), s_a.at[j, q], r_in.at[j, r, y, c], q * 4 + y * 2 + c)
+        return same(piece(j, r, y, c), s_a.at[j], r_col.at[j, r], q * 4 + y * 2 + c)
 
     def to_y(j, q):
-        return same(piece(j, q, y, c), s_y.at[j, q], r_in.at[j, q, y, c], o_y)
+        return same(piece(j, q, y, c), s_y.at[j], r_y.at[j, q], o_y)
 
     def to_core(j, q, u):
-        return same(piece(j, q, u, c), s_c.at[j, q, u], r_in.at[j, q, u, c], o_c)
-
-    def arrived(j, q, u, w):
-        same(piece(j, q, u, w), s_a.at[j, r], r_in.at[j, q, u, w], o_c).wait_recv()
+        return same(piece(j, q, u, c), s_c.at[j], r_core.at[j, u], o_c)
+
+    def arrived(j, q, u, w, recv):
+        same(piece(j, q, u, w), s_a.at[j], recv, o_c).wait_recv()
+
+    everyone = pl.ds(0, cols)
+    others = pl.ds(0, cols - 1)
+    both = pl.ds(0, 2)
 
     def crossing(half):
         tile = src.at[r, y, c, :, 2 * half]
@@ -244,7 +255,7 @@
         @pl.loop(1, cols)
         def _(d):
             q = (r + d) % cols
-            arrived(j, q, y, c)
+            arrived(j, q, y, c, r_col.at[j, q])
             to_y(j, q).start()
             to_core(j, q, y).start()
 
@@ -252,13 +263,11 @@
         @pl.loop(0, cols)
         def _(d):
             q = (r + d) % cols
-            arrived(j, q, 1 - y, c)
+            arrived(j, q, 1 - y, c, r_y.at[j, q])
             to_core(j, q, 1 - y).start()
 
     def other_core(j, u):
-        @pl.loop(0, cols)
-        def _(q):
-            arrived(j, q, u, 1 - c)
+        arrived(j, everyone, u, 1 - c, r_core.at[j, u])
 
     relay_column(0)
     relay_column(1)
@@ -336,16 +345,16 @@
 
     def pot_column(t, d):
         q = (r + d) % cols
-        return same(pot_at(t, r, y, c), t_a.at[t, q], t_in.at[t, r, y, c], q * 4 + y * 2 + c)
+        return same(pot_at(t, r, y, c), t_a.at[t], t_col.at[t, r], q * 4 + y * 2 + c)
 
     def pot_y(t, q):
-        return same(pot_at(t, q, y, c), t_y.at[t, q], t_in.at[t, q, y, c], o_y)
+        return same(pot_at(t, q, y, c), t_y.at[t], t_yin.at[t, q], o_y)
 
     def pot_core(t, q, u):
-        return same(pot_at(t, q, u, c), t_c.at[t, q, u], t_in.at[t, q, u, c], o_c)
-
-    def pot_arrived(t, q, u, w):
-        same(pot_at(t, q, u, w), t_a.at[t, r], t_in.at[t, q, u, w], o_c).wait_recv()
+        return same(pot_at(t, q, u, c), t_c.at[t], t_core.at[t, u], o_c)
+
+    def pot_arrived(t, q, u, w, recv):
+        same(pot_at(t, q, u, w), t_a.at[t], recv, o_c).wait_recv()
 
     def send_pots(t):
         @pl.loop(1, cols)
@@ -396,11 +405,11 @@
     gram_rows(0, value0)
     value1 = finish(1)
     gram_rows(1, value1)
-    gall[g, o] = gown[...]
+    gall[g * n_orb + o] = gown[...]
 
     def gram_to(d):
         flat = (o * 2 + g + d) % (2 * n_orb)
-        return copy(gown, gall.at[g, o], s_g.at[d], r_g.at[g, o], flat // 2, flat % 2)
+        return copy(gown, gall.at[g * n_orb + o], s_g, r_g, flat // 2, flat % 2)
 
     @pl.loop(1, 2 * n_orb)
     def _(d):
@@ -417,12 +426,14 @@
 
     write(pot_ref, 0, jnp.concatenate(value0[:2], axis=0))
     write(pot_ref, 1, jnp.concatenate(value1[:2], axis=0))
+    store_pot = pltpu.make_async_copy(pot_ref, pot_out, s_o.at[0])
+    store_pot.start()
 
     def pot_relay_column(t):
         @pl.loop(1, cols)
         def _(d):
             q = (r + d) % cols
-            pot_arrived(t, q, y, c)
+            pot_arrived(t, q, y, c, t_col.at[t, q])
             pot_y(t, q).start()
             pot_core(t, q, y).start()
 
@@ -430,7 +441,7 @@
         @pl.loop(0, cols)
         def _(d):
             q = (r + d) % cols
-            pot_arrived(t, q, 1 - y, c)
+            pot_arrived(t, q, 1 - y, c, t_yin.at[t, q])
             pot_core(t, q, 1 - y).start()
 
     pot_relay_column(0)
@@ -443,26 +454,17 @@
     for t in range(2):
         swap(t).wait_send()
 
-    @pl.loop(1, cols)
-    def _(d):
-        for j in range(3):
-            to_column(j, d).wait_send()
-
-    @pl.loop(0, cols)
-    def _(q):
-        for j in range(3):
-            to_y(j, q).wait_send()
-            for u in range(2):
-                to_core(j, q, u).wait_send()
-
-    @pl.loop(1, 2 * n_orb)
-    def _(d):
-        flat = (o * 2 + g + d) % (2 * n_orb)
-        there = gall.at[flat % 2, flat // 2]
-        copy(there, there, s_g.at[0], r_g.at[flat % 2, flat // 2], o_c, g).wait_recv()
+    for j in range(3):
+        same(piece(j, others, y, c), s_a.at[j], r_col.at[j, r], o_c).wait_send()
+        same(piece(j, everyone, y, c), s_y.at[j], r_col.at[j, r], o_c).wait_send()
+        same(piece(j, everyone, both, c), s_c.at[j], r_col.at[j, r], o_c).wait_send()
+
+    received = gall.at[pl.ds(0, 2 * n_orb - 1)]
+    grams = copy(received, received, s_g, r_g, o_c, g)
+    grams.wait_recv()
 
     def assemble(k, carry):
-        pairs = [gall[0, 4 * k + j] + gall[1, 4 * k + j] for j in range(4)]
+        pairs = [gall[4 * k + j] + gall[n_orb + 4 * k + j] for j in range(4)]
         start = 8 * k if isinstance(k, int) else pl.multiple_of(8 * k, 8)
         gmat[pl.ds(start, 8), :] = jnp.concatenate(pairs, axis=0)
         return carry
@@ -497,11 +499,9 @@
     inverse = right * (1.0 / jnp.sqrt(diag))
     a0, a1 = row_of(inverse, 2 * o), row_of(inverse, 2 * o + 1)
 
-    @pl.loop(0, cols)
-    def _(q):
-        for u in range(2):
-            for t in range(3):
-                pot_arrived(t, q, u, 1 - c)
+    for u in range(2):
+        for t in range(3):
+            pot_arrived(t, everyone, u, 1 - c, t_core.at[t, u])
 
     def add(k, sums):
         where = (k // 4, k % 4 // 2, k % 2)
@@ -522,22 +522,18 @@
     proj = loop(n_orb, add, (zero, zero))
     for t in range(2):
         write(proj_ref, t, jnp.concatenate(proj[t], axis=0))
-
-    @pl.loop(1, cols)
-    def _(d):
-        for t in range(3):
-            pot_column(t, d).wait_send()
-
-    @pl.loop(0, cols)
-    def _(q):
-        for t in range(3):
-            pot_y(t, q).wait_send()
-            for u in range(2):
-                pot_core(t, q, u).wait_send()
-
-    @pl.loop(1, 2 * n_orb)
-    def _(d):
-        gram_to(d).wait_send()
+    store_proj = pltpu.make_async_copy(proj_ref, proj_out, s_o.at[1])
+    store_proj.start()
+
+    for t in range(3):
+        same(pot_at(t, others, y, c), t_a.at[t], t_col.at[t, r], o_c).wait_send()
+        same(pot_at(t, everyone, y, c), t_y.at[t], t_col.at[t, r], o_c).wait_send()
+        same(pot_at(t, everyone, both, c), t_c.at[t], t_col.at[t, r], o_c).wait_send()
+
+    grams.wait_send()
+
+    store_pot.wait()
+    store_proj.wait()
 
 
 def on_device(orbitals, occupation):
@@ -554,8 +550,11 @@
         functools.partial(body, cols),
         out_shape=(full, full),
         in_specs=[vmem] * 2 + [pl.BlockSpec(memory_space=pl.ANY)] * 4,
-        out_specs=(vmem, vmem),
+        out_specs=(pl.BlockSpec(memory_space=pl.ANY),) * 2,
         scratch_shapes=[
+            pltpu.VMEM(orbitals.shape, f32),
+            pltpu.VMEM(orbitals.shape, f32),
+            dma((2,)),
             *[pltpu.VMEM(a.shape, a.dtype) for a in consts],
             pltpu.VMEM((cols, 2, 2, 2, 3, TILE, PLANE), bf16),
             pltpu.VMEM((2, 3, TILE, PLANE), f32),
@@ -566,23 +565,27 @@
             pltpu.VMEM((TILE, PLANE), bf16),
             pltpu.VMEM((2, n, LANES), f32),
             pltpu.VMEM((2, n), f32),
-            pltpu.VMEM((2, n_orb, 2, n), f32),
+            pltpu.VMEM((2 * n_orb, 2, n), f32),
             pltpu.VMEM((n, n), f32),
             dma((4,)),
             dma((2,)),
             dma((2,)),
+            dma((3,)),
+            dma((3,)),
+            dma((3,)),
             dma((3, cols)),
             dma((3, cols)),
-            dma((3, cols, 2)),
-            dma((3, cols, 2, 2)),
+            dma((3, 2)),
             dma((2,)),
             dma((2,)),
-            dma((2 * n_orb,)),
-            dma((2, n_orb)),
+            dma,
+            dma,
+            dma((3,)),
+            dma((3,)),
+            dma((3,)),
             dma((3, cols)),
             dma((3, cols)),
-            dma((3, cols, 2)),
-            dma((3, cols, 2, 2)),
+            dma((3, 2)),
         ],
         compiler_params=pltpu.CompilerParams(
             collective_id=0, has_side_effects=True, vmem_limit_bytes=60 * 1024 * 1024

time: 39.5 us -> 37.3 us (0.944)
  Pallas kernels: 36.5 us -> 34.3 us
    pallas_call x1, Pallas kernels: 36.5 us -> 34.3 us  [on_device(): pl.pallas_call(functools.partial(body, cols), out_shape=(full, full), in_...]
where the time goes in v5:
time: 37.3 us; the launch traced here: 37 us
  Pallas kernels  34.3 us (92%)
  local copies, waits for them, and re-layouts  2.05 us (5%)
  between operations  0.65 us (2%)
    pallas_call x1, Pallas kernels, on_device(): pl.pallas_call(functools.partial(body, cols), out_shape=(full, full), in_...  34.3 us
    unnamed x4, local copies, waits for them, and re-layouts  2.05 us

profile of v5, /device:TPU:0, one launch (start us, length us, event | category | flops | bytes accessed | tf_op | source)
XLA Modules:
  0.0 37.0 jit_solution(4613374981050874962)
XLA Ops:
  0.6 34.3 %exchange.1 = (f32[2,5760]{1,0:T(2,128)}, f32[2,5760]{1,0:T(2,128)}) custom-call(bf16[2,5760]{1,0:T(2,128)(2,1)} %own_ref.1, bf16[1,2]{1,0:T(2,128)(2,1)} %bitcast.1, bf16[192,192]{1,0:T(8,128)(2,1)} %constant.8.clone.tx_hbm, bf16[576,576]{1,0:T(8,128)(2,1)} %constant.9.clone.ty_hbm, bf16[384,384]{1,0:T(8,128)(2,1)} %constant.10.clone.tz_hbm, ...), custom_call_target="tpu_custom_call" | custom-call | tf_op jit(solution)/shard_map/exchange/pallas_call | solution.py:549
  34.9 0.0 copy-start
  35.0 1.4 %copy.10 = f32[2,5760]{1,0:T(2,128)} copy(f32[2,5760]{1,0:T(2,128)} %get-tuple-element.4) | data formatting | bytes 92160
  36.4 0.0 copy-done
  36.4 0.6 %copy.11 = f32[2,5760]{1,0:T(2,128)} copy(f32[2,5760]{1,0:T(2,128)S(1)} %copy-done) | data formatting | bytes 92160
Async XLA Ops:
  34.9 1.4 %copy-start = (f32[2,5760]{1,0:T(2,128)S(1)}, f32[2,5760]{1,0:T(2,128)}, u32[]{:S(2)}) copy-start(f32[2,5760]{1,0:T(2,128)} %get-tuple-element.5) | copy-start | bytes 138244

commit v6 on v5

--- a/solution.py
+++ b/solution.py
@@ -379,15 +379,7 @@
                 fold += jnp.concatenate([sums[:, PLANE - tail :], last], axis=1)
             rowsum[t, pl.ds(pl.multiple_of(q * 8, 8), 8), :] = fold
 
-        ones = jnp.ones((8, LANES), f32)
-        sums = lax.dot_general(
-            ones,
-            rowsum[t],
-            (((1,), (1,)), ((), ())),
-            precision=lax.Precision.HIGHEST,
-            preferred_element_type=f32,
-        )
-        gown[t : t + 1, :] = sums[0:1]
+        gown[t : t + 1, :] = jnp.sum(rowsum[t].T, axis=0, keepdims=True)
 
     def finish(t):
         swap(t).wait_recv()

time: 37.3 us -> 37.3 us (level)
  no operation moved by 1% of the time
where the time goes in v6:
time: 37.3 us; the launch traced here: 37 us
  Pallas kernels  34.3 us (92%)
  local copies, waits for them, and re-layouts  2.05 us (5%)
  between operations  0.65 us (2%)
    pallas_call x1, Pallas kernels, on_device(): pl.pallas_call(functools.partial(body, cols), out_shape=(full, full), in_...  34.3 us
    unnamed x4, local copies, waits for them, and re-layouts  2.05 us

profile of v6, /device:TPU:0, one launch (start us, length us, event | category | flops | bytes accessed | tf_op | source)
XLA Modules:
  0.0 37.0 jit_solution(7975996084186438335)
XLA Ops:
  0.6 34.3 %exchange.1 = (f32[2,5760]{1,0:T(2,128)}, f32[2,5760]{1,0:T(2,128)}) custom-call(bf16[2,5760]{1,0:T(2,128)(2,1)} %own_ref.1, bf16[1,2]{1,0:T(2,128)(2,1)} %bitcast.1, bf16[192,192]{1,0:T(8,128)(2,1)} %constant.8.clone.tx_hbm, bf16[576,576]{1,0:T(8,128)(2,1)} %constant.9.clone.ty_hbm, bf16[384,384]{1,0:T(8,128)(2,1)} %constant.10.clone.tz_hbm, ...), custom_call_target="tpu_custom_call" | custom-call | tf_op jit(solution)/shard_map/exchange/pallas_call | solution.py:541
  35.0 0.0 copy-start
  35.0 1.4 %copy.10 = f32[2,5760]{1,0:T(2,128)} copy(f32[2,5760]{1,0:T(2,128)} %get-tuple-element.4) | data formatting | bytes 92160
  36.4 0.0 copy-done
  36.4 0.6 %copy.11 = f32[2,5760]{1,0:T(2,128)} copy(f32[2,5760]{1,0:T(2,128)S(1)} %copy-done) | data formatting | bytes 92160
Async XLA Ops:
  35.0 1.4 %copy-start = (f32[2,5760]{1,0:T(2,128)S(1)}, f32[2,5760]{1,0:T(2,128)}, u32[]{:S(2)}) copy-start(f32[2,5760]{1,0:T(2,128)} %get-tuple-element.5) | copy-start | bytes 138244

commit v7 on v6

--- a/solution.py
+++ b/solution.py
@@ -396,6 +396,7 @@
     other_core(2, 1 - y)
     gram_rows(0, value0)
     value1 = finish(1)
+    send_pots(1)
     gram_rows(1, value1)
     gall[g * n_orb + o] = gown[...]
 
@@ -408,7 +409,6 @@
         gram_to(d).start()
 
     pedge[r, y, c] = jnp.concatenate([value0[1], value1[1]], axis=0)
-    send_pots(1)
     send_pots(2)
 
     def write(ref, t, value):

time: 37.3 us -> 37 us (level)
  no operation moved by 1% of the time
where the time goes in v7:
time: 37 us; the launch traced here: 36.8 us
  Pallas kernels  34.1 us (92%)
  local copies, waits for them, and re-layouts  2.05 us (6%)
  between operations  0.65 us (2%)
    pallas_call x1, Pallas kernels, on_device(): pl.pallas_call(functools.partial(body, cols), out_shape=(full, full), in_...  34.1 us
    unnamed x4, local copies, waits for them, and re-layouts  2.05 us

profile of v7, /device:TPU:0, one launch (start us, length us, event | category | flops | bytes accessed | tf_op | source)
XLA Modules:
  0.0 36.8 jit_solution(9333647089368861521)
XLA Ops:
  0.6 34.1 %exchange.1 = (f32[2,5760]{1,0:T(2,128)}, f32[2,5760]{1,0:T(2,128)}) custom-call(bf16[2,5760]{1,0:T(2,128)(2,1)} %own_ref.1, bf16[1,2]{1,0:T(2,128)(2,1)} %bitcast.1, bf16[192,192]{1,0:T(8,128)(2,1)} %constant.8.clone.tx_hbm, bf16[576,576]{1,0:T(8,128)(2,1)} %constant.9.clone.ty_hbm, bf16[384,384]{1,0:T(8,128)(2,1)} %constant.10.clone.tz_hbm, ...), custom_call_target="tpu_custom_call" | custom-call | tf_op jit(solution)/shard_map/exchange/pallas_call | solution.py:541
  34.7 0.0 copy-start
  34.7 1.4 %copy.10 = f32[2,5760]{1,0:T(2,128)} copy(f32[2,5760]{1,0:T(2,128)} %get-tuple-element.4) | data formatting | bytes 92160
  36.1 0.0 copy-done
  36.1 0.6 %copy.11 = f32[2,5760]{1,0:T(2,128)} copy(f32[2,5760]{1,0:T(2,128)S(1)} %copy-done) | data formatting | bytes 92160
Async XLA Ops:
  34.7 1.4 %copy-start = (f32[2,5760]{1,0:T(2,128)S(1)}, f32[2,5760]{1,0:T(2,128)}, u32[]{:S(2)}) copy-start(f32[2,5760]{1,0:T(2,128)} %get-tuple-element.5) | copy-start | bytes 138244
